TPU v7x, 128 devices: a whole 4x4x4 slice. The times are simulated.
128 devices in a mesh: traj: 4 (over y), grid: 32 (over x, z, core).
Axes of the slice: x: 4, y: 4, z: 4, core: 2. Of those that a mesh axis runs over, the one named last changes fastest.
Arguments:
- psi_modes: float32 [4, 2, 256, 256, 256], P('traj', None, None, 'grid'), may hold values from -6 to 6
- noise: float32 [4, 2, 256, 256, 256], P('traj', None, 'grid'), may hold values from -6 to 6
- mask: int32 [256, 256, 256], P(None, 'grid'), may hold values from 0 to 1, as said below
Outputs:
- psi_next: float32 [4, 2, 256, 256, 256], P('traj', None, None, 'grid')
- momentum_hist: float32 [128], replicated
Inputs may be any that keep to these rules, and one draw needn't show every extreme that they name: mask is 0 at every mode whose signed third index has magnitude 256/4 or more, and 1 at some mode whose signed third index has magnitude 256/4 - 1.
All inputs are finite; a program needn't handle non-finite values.
Results may differ from a plain program's by a relative error of at most 0.00023.
Values sent between devices are 32-bit elements; how exact they have to be, the bound alone decides.
No kernel may reach another device: no remote copies, remote signals or barrier semaphores. Data moves between devices by JAX's collectives and lax.ppermute only.
A program may use at most 128 MiB of HBM per device.

v0:
```python
import jax
import jax.numpy as jnp
import numpy as np
from jax import lax
from jax.experimental import pallas as pl
from jax.experimental.pallas import tpu as pltpu
from jax.sharding import PartitionSpec as P

SHELLS = 128
N = 256
GRID = 32
LOC = N // GRID
ZM = N // 2
TRAJ = 4

time_step = 1.0
damping = 0.05
coupling = 10.0
chem_potential = 1.0
noise_amp = 0.1
trap_strength = 8.0

F32 = jnp.float32
BF16 = jnp.bfloat16

RESIDUES = sorted({(s * s) % 64 for s in range(64)})

SIN_C = (0.9999999957052124, -0.1666665795268036, 0.008333050198586583, -0.00019809014686181177, 2.6050929465880504e-06)
COS_C = (0.9999999997792474, -0.49999999355360947, 0.0416666361485972, -0.001388836006030289, 2.476009476594345e-05, -2.6050342497228447e-07)
PI_HI = 3.140625
PI_LO = float(np.pi - 3.140625)
TRIG_MAX = 4000.0


def host_tables():
    index = np.arange(N)
    signed = np.where(index < N // 2, index, index - N)
    wave = signed * (2.0 * np.pi / N)
    step = np.exp(-(damping + 1j) * 0.25 * time_step * wave**2)
    phase = np.exp(2j * np.pi * ((index[:, None] * index[None, :]) % N) / N) / np.sqrt(N)
    inverse = phase * step[None, :]
    forward = np.conj(phase) * step[:, None]
    cols = np.concatenate([index[: N // 4], index[3 * N // 4 :]])
    inv_tall = np.concatenate([inverse.real, inverse.imag], 0)
    fwd_tall = np.concatenate([forward.real, forward.imag], 0)
    iz = inverse[:, cols].T
    inv_z = np.block([[iz.real, iz.imag], [-iz.imag, iz.real]])
    fz = forward[cols, :].T
    fwd_z = np.block([[fz.real, fz.imag], [-fz.imag, fz.real]])
    return inv_tall, fwd_tall, inv_z, fwd_z


def halves(table):
    table = np.asarray(table, np.float32)
    high = table.astype(BF16)
    low = (table - high.astype(np.float32)).astype(BF16)
    return jnp.asarray(high), jnp.asarray(low)


def split(value):
    high = value.astype(BF16)
    return high, (value - high.astype(F32)).astype(BF16)


def dot(left, right):
    return jnp.dot(left, right, preferred_element_type=F32)


def dot3(left, right):
    return dot(left[0], right[0]) + dot(left[0], right[1]) + dot(left[1], right[0])


def column_transform(table, real, imag):
    count = real.shape[1]
    both = dot3(table, split(jnp.concatenate([real, imag], axis=1)))
    top, low = both[:N], both[N:]
    return top[:, :count] - low[:, count:], top[:, count:] + low[:, :count]


def select_tiles(values):
    lane = lax.broadcasted_iota(jnp.int32, values.shape[:-1] + (ZM,), values.ndim - 1)
    return jnp.where(lane < ZM // 2, values[..., :ZM], values[..., ZM:])


def first_kernel(psi_ref, mask_ref, hi_ref, lo_ref, out_ref, field):
    keep = select_tiles(mask_ref[...]).astype(F32)
    for part in range(2):
        field[part] = (select_tiles(psi_ref[0, part]) * keep).reshape(N * LOC, ZM)
    table = (hi_ref[...], lo_ref[...])
    for row in range(LOC):
        real, imag = column_transform(
            table, field[0, pl.ds(row, N, stride=LOC), :], field[1, pl.ds(row, N, stride=LOC), :]
        )
        out_ref[pl.ds(row, N, stride=2 * LOC), :] = real
        out_ref[pl.ds(LOC + row, N, stride=2 * LOC), :] = imag


def plane_kernel(
    rank_ref, in_ref, noise_ref, iy_hi, iy_lo, iz_hi, iz_lo, fz_hi, fz_lo, fy_hi, fy_lo, out_ref, base
):
    step = pl.program_id(0)

    @pl.when(step == 0)
    def _():
        shape = (N, N)
        pos_y = (lax.broadcasted_iota(jnp.int32, shape, 0).astype(F32) + 0.5) / N - 0.5
        pos_z = (lax.broadcasted_iota(jnp.int32, shape, 1).astype(F32) + 0.5) / N - 0.5
        base[...] = trap_strength * (pos_y * pos_y + pos_z * pos_z) - chem_potential

    pos_x = ((rank_ref[0] * LOC + step).astype(F32) + 0.5) / N - 0.5
    shift_x = trap_strength * pos_x * pos_x

    real = in_ref[:, 0, 0].reshape(N, ZM)
    imag = in_ref[:, 0, 1].reshape(N, ZM)
    real, imag = column_transform((iy_hi[...], iy_lo[...]), real, imag)
    both = dot3(split(jnp.concatenate([real, imag], axis=1)), (iz_hi[...], iz_lo[...]))
    real, imag = both[:, :N], both[:, N:]
    energy = base[...] + shift_x + coupling * (real * real + imag * imag)
    angle = jnp.minimum(energy * time_step, TRIG_MAX)
    turns = jnp.round(angle * (1.0 / np.pi))
    rest = (angle - turns * PI_HI) - turns * PI_LO
    square = rest * rest
    sine = SIN_C[-1]
    for coef in SIN_C[-2::-1]:
        sine = sine * square + coef
    cosine = COS_C[-1]
    for coef in COS_C[-2::-1]:
        cosine = cosine * square + coef
    half = turns * 0.5
    sign = 1.0 - 4.0 * (half - jnp.floor(half))
    decay = jnp.exp(energy * (-damping * time_step)) * sign
    evo_real = decay * cosine
    evo_imag = decay * (sine * rest)
    moved_real = real * evo_real + imag * evo_imag + noise_amp * noise_ref[0, 0, 0]
    moved_imag = imag * evo_real - real * evo_imag + noise_amp * noise_ref[0, 1, 0]
    both = dot3(split(jnp.concatenate([moved_real, moved_imag], axis=1)), (fz_hi[...], fz_lo[...]))
    real, imag = column_transform((fy_hi[...], fy_lo[...]), both[:, :ZM], both[:, ZM:])
    out_ref[:, 0, 0] = real.reshape(GRID, LOC, ZM)
    out_ref[:, 0, 1] = imag.reshape(GRID, LOC, ZM)


def last_kernel(rank_ref, in_ref, mask_ref, hi_ref, lo_ref, out_ref, hist_ref, keep, field, occ_hi, occ_lo):
    keep[...] = select_tiles(mask_ref[...]).astype(F32).reshape(N * LOC, ZM)
    table = (hi_ref[...], lo_ref[...])
    for row in range(LOC):
        real, imag = column_transform(
            table,
            in_ref[pl.ds(row, N, stride=2 * LOC), :],
            in_ref[pl.ds(LOC + row, N, stride=2 * LOC), :],
        )
        mask = keep[pl.ds(row, N, stride=LOC), :]
        real = real * mask
        imag = imag * mask
        field[0, pl.ds(row, N, stride=LOC), :] = real
        field[1, pl.ds(row, N, stride=LOC), :] = imag
        high, low = split(real * real + imag * imag)
        occ_hi[:, row * ZM : (row + 1) * ZM] = high
        occ_lo[:, row * ZM : (row + 1) * ZM] = low
    lane = lax.broadcasted_iota(jnp.int32, (N, LOC, ZM), 2)
    for part in range(2):
        value = field[part].reshape(N, LOC, ZM)
        out_ref[0, part, :, :, :ZM] = jnp.where(lane < ZM // 2, value, 0.0)
        out_ref[0, part, :, :, ZM:] = jnp.where(lane < ZM // 2, 0.0, value)

    shape = (LOC * ZM, SHELLS)
    place = lax.broadcasted_iota(jnp.int32, shape, 0)
    index_y = rank_ref[0] * LOC + (place >> 7)
    index_z = place & (ZM - 1)
    sig_y = jnp.where(index_y < N // 2, index_y, index_y - N)
    sig_z = jnp.where(index_z < ZM // 2, index_z, index_z - ZM)
    rest = jnp.minimum(sig_y * sig_y + sig_z * sig_z, 64 * (SHELLS - 1))
    gap = rest - 64 * lax.broadcasted_iota(jnp.int32, shape, 1)
    shape = (N, SHELLS)
    index_x = lax.broadcasted_iota(jnp.int32, shape, 0)
    sig_x = jnp.where(index_x < N // 2, index_x, index_x - N)
    square_x = sig_x * sig_x
    residue = square_x & 63
    sums = jnp.zeros(shape, F32)
    for first in range(0, len(RESIDUES), 2):
        pair = RESIDUES[first : first + 2]
        hits = jnp.concatenate(
            [jnp.where((gap >= -r) & (gap < 64 - r), 1.0, 0.0).astype(BF16) for r in pair], axis=1
        )
        found = dot(occ_hi[...], hits) + dot(occ_lo[...], hits)
        for place_of, r in enumerate(pair):
            sums = jnp.where(residue == r, found[:, place_of * SHELLS : (place_of + 1) * SHELLS], sums)
    moves = square_x >> 6
    bins = lax.broadcasted_iota(jnp.int32, shape, 1)
    far = moves >= SHELLS - 1
    over = jnp.where(far, sums, 0.0)
    sums = jnp.where(far, 0.0, sums)
    for bit in range(7):
        width = 1 << bit
        chosen = (moves & width) != 0
        past = chosen & (bins >= SHELLS - width)
        over = over + jnp.where(past, sums, 0.0)
        rolled = jnp.where(bins >= width, pltpu.roll(sums, width, 1), 0.0)
        sums = jnp.where(chosen, rolled, sums)
    total = jnp.sum(sums, axis=0, keepdims=True)
    extra = jnp.sum(jnp.sum(over, axis=0, keepdims=True), axis=1, keepdims=True)
    hist_ref[...] = total + jnp.where(bins[:1] == SHELLS - 1, extra, 0.0)


def params(mib):
    return pltpu.CompilerParams(vmem_limit_bytes=mib * 1024 * 1024)


def whole(shape):
    return pl.BlockSpec(shape, lambda *_: (0,) * len(shape))


def exchange(value):
    return lax.all_to_all(value, "grid", split_axis=0, concat_axis=0, tiled=True)


def summed_over(value, axis):
    copies = jnp.broadcast_to(value, (lax.axis_size(axis), *value.shape))
    return jnp.sum(lax.all_to_all(copies, axis, split_axis=0, concat_axis=0, tiled=True), axis=0)


def shards(psi_modes, noise, mask):
    inv_tall, fwd_tall, inv_z, fwd_z = (halves(table) for table in host_tables())
    rank = lax.axis_index("grid").astype(jnp.int32).reshape(1)
    tall = [whole((2 * N, N))] * 2
    smem = pl.BlockSpec(memory_space=pltpu.SMEM)
    rows = GRID * LOC * 2 * LOC
    message = (GRID, LOC, 2, LOC, ZM)
    sent = pl.pallas_call(
        first_kernel,
        out_shape=jax.ShapeDtypeStruct((rows, ZM), F32),
        grid=(1,),
        in_specs=[whole((1, 2, N, LOC, N)), whole((N, LOC, N)), *tall],
        out_specs=whole((rows, ZM)),
        scratch_shapes=[pltpu.VMEM((2, N * LOC, ZM), F32)],
        compiler_params=params(48),
        name="first",
    )(psi_modes, mask, *inv_tall)
    planes = exchange(sent.reshape(message))
    block = pl.BlockSpec((GRID, 1, 2, LOC, ZM), lambda i: (0, i, 0, 0, 0))
    sent = pl.pallas_call(
        plane_kernel,
        out_shape=jax.ShapeDtypeStruct(message, F32),
        grid=(LOC,),
        in_specs=[
            smem,
            block,
            pl.BlockSpec((1, 2, 1, N, N), lambda i: (0, 0, i, 0, 0)),
            *tall,
            *[whole((N, 2 * N))] * 2,
            *tall,
            *tall,
        ],
        out_specs=block,
        scratch_shapes=[pltpu.VMEM((N, N), F32)],
        compiler_params=params(48),
        name="planes",
    )(rank, planes, noise, *inv_tall, *inv_z, *fwd_z, *fwd_tall)
    rows_in = exchange(sent).reshape(rows, ZM)
    psi_next, hist = pl.pallas_call(
        last_kernel,
        out_shape=(
            jax.ShapeDtypeStruct(psi_modes.shape, F32),
            jax.ShapeDtypeStruct((1, SHELLS), F32),
        ),
        grid=(1,),
        in_specs=[smem, whole((rows, ZM)), whole((N, LOC, N)), *tall],
        out_specs=(whole((1, 2, N, LOC, N)), whole((1, SHELLS))),
        scratch_shapes=[
            pltpu.VMEM((N * LOC, ZM), F32),
            pltpu.VMEM((2, N * LOC, ZM), F32),
            pltpu.VMEM((N, LOC * ZM), BF16),
            pltpu.VMEM((N, LOC * ZM), BF16),
        ],
        compiler_params=params(56),
        name="last",
    )(rank, rows_in, mask, *fwd_tall)
    hist = summed_over(summed_over(hist, "grid"), "traj")
    return psi_next, hist.reshape(SHELLS) * (SHELLS / (TRAJ * N * N * N))


def solution(mesh):
    placed = (
        P("traj", None, None, "grid", None),
        P("traj", None, "grid", None, None),
        P(None, "grid", None),
    )
    return jax.shard_map(
        shards,
        mesh=mesh,
        in_specs=placed,
        out_specs=(P("traj", None, None, "grid", None), P()),
        check_vma=False,
    )
```

profile of v0, /device:TPU:0, one launch (start us, length us, event | category | flops | bytes accessed | tf_op | source)
XLA Modules:
  0.0 130.6 jit_solution(7598149840875880918)
XLA Ops:
  0.6 0.0 copy-start
  0.6 1.6 %copy-done = s32[256,8,256]{2,1,0:T(8,128)S(1)} copy-done((s32[256,8,256]{2,1,0:T(8,128)S(1)}, s32[256,8,256]{2,1,0:T(8,128)}, u32[]{:S(2)}) %copy-start) | copy-done | bytes 2097176
  2.2 0.0 copy-start.3
  2.2 0.9 copy-done.3
  3.2 0.0 copy-start.5
  3.2 0.9 copy-done.5
  4.1 6.1 %first.1 = f32[4096,128]{1,0:T(8,128)} custom-call(f32[1,2,256,8,256]{4,3,2,1,0:T(8,128)} %psi_ref.1, s32[256,8,256]{2,1,0:T(8,128)S(1)} %copy-done, bf16[512,256]{1,0:T(8,128)(2,1)S(1)} %copy-done.5, bf16[512,256]{1,0:T(8,128)(2,1)S(1)} %copy-done.3), custom_call_target="tpu_custom_call" | custom-call | tf_op jit(solution)/shard_map/first/pallas_call | solution.py:228
  10.2 0.0 copy-start.1
  10.2 0.0 copy-start.2
  10.2 0.0 copy-start.4
  10.2 0.0 copy-start.6
  10.2 0.0 copy-start.7
  10.3 0.0 copy-start.8
  10.3 0.0 copy-start.9
  10.3 0.0 copy-start.10
  10.3 8.5 %all-to-all-start = ((f32[32,8,2,8,128]{4,3,2,1,0:T(8,128)}), f32[32,8,2,8,128]{4,3,2,1,0:T(8,128)}, u32[]{:S(2)}, u32[]{:S(2)}) async-start(f32[32,8,2,8,128]{4,3,2,1,0:T(8,128)} %bitcast.1), calls=%async_computation | async-start | bytes 4194304 | tf_op jit(solution)/shard_map/all_to_all | solution.py:213
  18.9 28.9 %all-to-all-done.in_ref = f32[32,8,2,8,128]{4,3,2,1,0:T(8,128)} async-done(((f32[32,8,2,8,128]{4,3,2,1,0:T(8,128)}), f32[32,8,2,8,128]{4,3,2,1,0:T(8,128)}, u32[]{:S(2)}, u32[]{:S(2)}) %all-to-all-start) | async-done | bytes 2097184 | tf_op jit(solution)/shard_map/all_to_all | solution.py:213
  47.8 0.0 copy-done.1
  47.8 0.0 copy-done.2
  47.8 0.0 copy-done.4
  47.8 0.0 copy-done.6
  47.8 0.0 copy-done.7
  47.8 0.0 copy-done.8
  47.8 0.0 copy-done.9
  47.8 0.0 copy-done.10
  47.8 20.6 %planes.1 = f32[32,8,2,8,128]{4,3,2,1,0:T(8,128)S(1)} custom-call(s32[1]{0:T(128)} %bitcast.rank_ref, f32[32,8,2,8,128]{4,3,2,1,0:T(8,128)} %all-to-all-done.in_ref, f32[1,2,8,256,256]{4,3,2,1,0:T(8,128)} %noise_ref.1, bf16[512,256]{1,0:T(8,128)(2,1)S(1)} %copy-done.6, bf16[512,256]{1,0:T(8,128)(2,1)S(1)} %copy-done.4, bf16[256,512]{1,0:T(8,128)(2,1)S(1)} %copy-done.10, ...), custom_call_target="tpu_custom_call" | custom-call | tf_op jit(solution)/shard_map/planes/pallas_call | solution.py:240
  68.4 31.7 %all_to_all.20 = f32[32,8,2,8,128]{4,3,2,1,0:T(8,128)} all-to-all(f32[32,8,2,8,128]{4,3,2,1,0:T(8,128)S(1)} %planes.1), channel_id=1, replica_groups=mesh['traj'=4,'grid'=32] {'grid'}, dimensions={0} | all-to-all | bytes 4194304 | tf_op jit(solution)/shard_map/all_to_all | solution.py:213
  100.1 8.4 %last.1 = (f32[1,2,256,8,256]{4,3,2,1,0:T(8,128)}, f32[1,128]{1,0:T(1,128)}) custom-call(s32[1]{0:T(128)} %bitcast.rank_ref, f32[4096,128]{1,0:T(8,128)} %bitcast.6, s32[256,8,256]{2,1,0:T(8,128)} %mask_ref.3, bf16[512,256]{1,0:T(8,128)(2,1)} %constant.26.clone.fy_hi.hi_ref, bf16[512,256]{1,0:T(8,128)(2,1)} %constant.27.clone.fy_lo.lo_ref), custom_call_target="tpu_custom_call" | custom-call | tf_op jit(solution)/shard_map/last/pallas_call | solution.py:259
  108.5 0.7 broadcast_in_dim.6
  109.2 11.2 %all_to_all.21 = f32[32,1,128]{2,1,0:T(1,128)S(1)} all-to-all(f32[32,1,128]{2,1,0:T(1,128)S(1)} %broadcast_in_dim.6), channel_id=1, replica_groups=mesh['traj'=4,'grid'=32] {'grid'}, dimensions={0} | all-to-all | bytes 32768 | tf_op jit(solution)/shard_map/all_to_all | solution.py:218
  120.5 9.5 %all_to_all.22 = f32[4,1,128]{2,1,0:T(1,128)S(1)} all-to-all(f32[4,1,128]{2,1,0:T(1,128)S(1)} %broadcast_in_dim.7), channel_id=1, replica_groups=mesh['traj'=4,'grid'=32] {'traj'}, dimensions={0} | all-to-all | bytes 4096 | tf_op jit(solution)/shard_map/all_to_all | solution.py:218
  130.0 0.5 broadcast_multiply_fusion
  (3 shorter events, 0.0 us)
Async XLA Ops:
  0.6 1.6 %copy-start = (s32[256,8,256]{2,1,0:T(8,128)S(1)}, s32[256,8,256]{2,1,0:T(8,128)}, u32[]{:S(2)}) copy-start(s32[256,8,256]{2,1,0:T(8,128)} %mask_ref.3) | copy-start | bytes 6291460
  2.2 0.9 copy-start.3
  3.2 0.9 copy-start.5
  10.2 37.5 %copy-start.1 = (bf16[512,256]{1,0:T(8,128)(2,1)S(1)}, bf16[512,256]{1,0:T(8,128)(2,1)}, u32[]{:S(2)}) copy-start(bf16[512,256]{1,0:T(8,128)(2,1)} %constant.27.clone.fy_lo.lo_ref) | copy-start | bytes 786436
  10.2 37.5 %copy-start.2 = (bf16[512,256]{1,0:T(8,128)(2,1)S(1)}, bf16[512,256]{1,0:T(8,128)(2,1)}, u32[]{:S(2)}) copy-start(bf16[512,256]{1,0:T(8,128)(2,1)} %constant.26.clone.fy_hi.hi_ref) | copy-start | bytes 786436
  10.2 37.5 %copy-start.4 = (bf16[512,256]{1,0:T(8,128)(2,1)S(1)}, bf16[512,256]{1,0:T(8,128)(2,1)}, u32[]{:S(2)}) copy-start(bf16[512,256]{1,0:T(8,128)(2,1)} %constant.25.clone.lo_ref.iy_lo) | copy-start | bytes 786436
  10.2 37.5 %copy-start.6 = (bf16[512,256]{1,0:T(8,128)(2,1)S(1)}, bf16[512,256]{1,0:T(8,128)(2,1)}, u32[]{:S(2)}) copy-start(bf16[512,256]{1,0:T(8,128)(2,1)} %constant.24.clone.hi_ref.iy_hi) | copy-start | bytes 786436
  10.2 37.5 %copy-start.7 = (bf16[512,256]{1,0:T(8,128)(2,1)S(1)}, bf16[512,256]{1,0:T(8,128)(2,1)}, u32[]{:S(2)}) copy-start(bf16[512,256]{1,0:T(8,128)(2,1)} %constant.31.clone.fz_lo) | copy-start | bytes 786436
  10.3 37.5 %copy-start.8 = (bf16[512,256]{1,0:T(8,128)(2,1)S(1)}, bf16[512,256]{1,0:T(8,128)(2,1)}, u32[]{:S(2)}) copy-start(bf16[512,256]{1,0:T(8,128)(2,1)} %constant.30.clone.fz_hi) | copy-start | bytes 786436
  10.3 37.5 %copy-start.9 = (bf16[256,512]{1,0:T(8,128)(2,1)S(1)}, bf16[256,512]{1,0:T(8,128)(2,1)}, u32[]{:S(2)}) copy-start(bf16[256,512]{1,0:T(8,128)(2,1)} %constant.29.clone.iz_lo) | copy-start | bytes 786436
  10.3 37.5 %copy-start.10 = (bf16[256,512]{1,0:T(8,128)(2,1)S(1)}, bf16[256,512]{1,0:T(8,128)(2,1)}, u32[]{:S(2)}) copy-start(bf16[256,512]{1,0:T(8,128)(2,1)} %constant.28.clone.iz_hi) | copy-start | bytes 786436
  10.3 37.5 %all-to-all-start = ((f32[32,8,2,8,128]{4,3,2,1,0:T(8,128)}), f32[32,8,2,8,128]{4,3,2,1,0:T(8,128)}, u32[]{:S(2)}, u32[]{:S(2)}) async-start(f32[32,8,2,8,128]{4,3,2,1,0:T(8,128)} %bitcast.1), calls=%async_computation | async-start | bytes 4194304 | tf_op jit(solution)/shard_map/all_to_all | solution.py:213
where the time goes:
time: 131 us
  blocking collectives  52.5 us (40%)
  Pallas kernels  35.1 us (27%)
  waiting for transfers between devices  28.9 us (22%)
  starting transfers between devices  8.55 us (7%)
  local copies, waits for them, and re-layouts  4.21 us (3%)
    all_to_all x1, blocking collectives, exchange(): lax.all_to_all(value, 'grid', split_axis=0, concat_axis=0, tiled=True)  31.7 us
    all_to_all x1, waiting for transfers between devices, exchange(): lax.all_to_all(value, 'grid', split_axis=0, concat_axis=0, tiled=True)  28.9 us
    all_to_all x2, blocking collectives, summed_over(): lax.all_to_all(copies, axis, split_axis=0, concat_axis=0, tiled=True)  20.8 us
    pallas_call x1, Pallas kernels, shards(): pl.pallas_call(plane_kernel, out_shape=jax.ShapeDtypeStruct(message, F32)...  20.6 us
    all_to_all x1, starting transfers between devices, exchange(): lax.all_to_all(value, 'grid', split_axis=0, concat_axis=0, tiled=True)  8.55 us
    pallas_call x1, Pallas kernels, shards(): pl.pallas_call(last_kernel, out_shape=(jax.ShapeDtypeStruct(psi_modes.sha...  8.39 us
    pallas_call x1, Pallas kernels, shards(): pl.pallas_call(first_kernel, out_shape=jax.ShapeDtypeStruct((rows, ZM), F...  6.11 us
    unnamed x22, local copies, waits for them, and re-layouts  3.53 us
  transfers between devices with their start and end apart: 1, of which 1 were waited for; matrix products, arithmetic and copies ran while one was open for 0% of the time, Pallas kernels for 0%

commit v1 on v0

v1 whole, which is shorter than its diff:
```python
import jax
import jax.numpy as jnp
import numpy as np
from jax import lax
from jax.experimental import pallas as pl
from jax.experimental.pallas import tpu as pltpu
from jax.sharding import PartitionSpec as P

SHELLS = 128
N = 256
GRID = 32
LOC = N // GRID
ZM = N // 2
TRAJ = 4
PLANES_MIB = 48
STEP_PLANES = 2

time_step = 1.0
damping = 0.05
coupling = 10.0
chem_potential = 1.0
noise_amp = 0.1
trap_strength = 8.0

F32 = jnp.float32
BF16 = jnp.bfloat16

RESIDUES = sorted({(s * s) % 64 for s in range(64)})
NEAR = 96
GAP_MAX = 100.0

SIN_C = [
    c * np.sqrt(2.0) * np.pi ** (2 * k + 1)
    for k, c in enumerate((0.9999999957052124, -0.1666665795268036, 0.008333050198586583, -0.00019809014686181177, 2.6050929465880504e-06))
]
COS_C = [
    c * np.sqrt(2.0) * np.pi ** (2 * k)
    for k, c in enumerate((0.9999999531318189, -0.49999904875147083, 0.041663574368409804, -0.0013853632426514488, 2.3152375214584864e-05))
]
TURN = time_step / (2.0 * np.pi)
DECAY_LOG2 = -damping * 2.0 * np.pi / np.log(2.0)
AMP_LOG2 = -np.log2(noise_amp)


def host_tables():
    index = np.arange(N)
    signed = np.where(index < N // 2, index, index - N)
    wave = signed * (2.0 * np.pi / N)
    step = np.exp(-(damping + 1j) * 0.25 * time_step * wave**2)
    phase = np.exp(2j * np.pi * ((index[:, None] * index[None, :]) % N) / N) / np.sqrt(N)
    inverse = phase * step[None, :]
    forward = np.conj(phase) * step[:, None]
    cols = np.concatenate([index[: N // 4], index[3 * N // 4 :]])
    inv_tall = np.concatenate([inverse.real, inverse.imag], 0)
    fwd_tall = np.concatenate([forward.real, forward.imag], 0)
    iz = inverse[:, cols].T
    inv_z = np.concatenate([iz.real, -iz.imag, iz.imag, iz.real], 0)
    fz = noise_amp * forward[cols, :].T
    fwd_z = np.block([[fz.real, fz.imag], [-fz.imag, fz.real]])
    return inv_tall, fwd_tall, inv_z, fwd_z


def halves(table):
    table = np.asarray(table, np.float32)
    high = table.astype(BF16)
    low = (table - high.astype(np.float32)).astype(BF16)
    return np.stack([high, low])


def split(value):
    high = value.astype(BF16)
    return high, (value - high.astype(F32)).astype(BF16)


def dot(left, right):
    return jnp.dot(left, right, preferred_element_type=F32)


def dot3(left, right):
    return dot(left[0], right[0]) + dot(left[0], right[1]) + dot(left[1], right[0])


def column_transform(table, real, imag):
    count = real.shape[1]
    both = dot3(table, split(jnp.concatenate([real, imag], axis=1)))
    top, low = both[:N], both[N:]
    return top[:, :count] - low[:, count:], top[:, count:] + low[:, :count]


def select_tiles(values):
    lane = lax.broadcasted_iota(jnp.int32, values.shape[:-1] + (ZM,), values.ndim - 1)
    return jnp.where(lane < ZM // 2, values[..., :ZM], values[..., ZM:])


def polynomial(coefs, square):
    value = coefs[-1]
    for coef in coefs[-2::-1]:
        value = value * square + coef
    return value


def first_kernel(psi_hbm, mask_hbm, table_hbm, out_ref, psi, mask, table_ref, field, sems):
    pieces = 4
    rows = N // pieces
    copies = []
    for piece in range(pieces):
        part = pl.ds(piece * rows, rows)
        copies.append(
            (
                pltpu.make_async_copy(psi_hbm.at[0, :, part], psi.at[:, part], sems.at[0, piece]),
                pltpu.make_async_copy(mask_hbm.at[part], mask.at[part], sems.at[1, piece]),
            )
        )
    tables = [pltpu.make_async_copy(table_hbm.at[pl.ds(0, 2)], table_ref, sems.at[2, 0])]
    for pair in copies:
        for copy in pair:
            copy.start()
    for copy in tables:
        copy.start()
    for piece, pair in enumerate(copies):
        for copy in pair:
            copy.wait()
        part = slice(piece * rows, (piece + 1) * rows)
        keep = select_tiles(mask[part]).astype(F32)
        for half in range(2):
            field[half, piece * rows * LOC : (piece + 1) * rows * LOC] = (
                select_tiles(psi[half, part]) * keep
            ).reshape(rows * LOC, ZM)
    for copy in tables:
        copy.wait()
    table = (table_ref[0], table_ref[1])
    for row in range(LOC):
        real, imag = column_transform(
            table, field[0, pl.ds(row, N, stride=LOC), :], field[1, pl.ds(row, N, stride=LOC), :]
        )
        out_ref[:, 0, row] = real.reshape(GRID, LOC, ZM)
        out_ref[:, 1, row] = imag.reshape(GRID, LOC, ZM)


def plane_kernel(
    rank_ref, in_ref, noise_hbm, tables_hbm, out_ref, base, noise_ref, tables, first_field, second_field, sems
):
    step = pl.program_id(0)
    groups = LOC // STEP_PLANES
    table_copies = [
        pltpu.make_async_copy(tables_hbm.at[part], tables.at[part], sems.at[groups + k])
        for k, part in enumerate((pl.ds(0, 2), pl.ds(2, 2), pl.ds(4, 4)))
    ]

    def noise_copy(group):
        planes = pl.ds(group * STEP_PLANES, STEP_PLANES)
        return pltpu.make_async_copy(noise_hbm.at[0, :, planes], noise_ref.at[:, planes], sems.at[group])

    def to_field(group, field):
        lanes = []
        for inner in range(STEP_PLANES):
            rows = pl.ds(group * STEP_PLANES + inner, LOC, stride=LOC)
            real = jnp.concatenate([in_ref[g, 0, rows, :] for g in range(GRID)], axis=0)
            imag = jnp.concatenate([in_ref[g, 1, rows, :] for g in range(GRID)], axis=0)
            real, imag = column_transform((tables[0], tables[1]), real, imag)
            lanes.append(jnp.concatenate([real, imag], axis=1))
        value = split(jnp.concatenate(lanes, axis=0))
        for part in range(2):
            lines = pl.ds(part * N, N)
            field[part] = dot3(value, (tables[2, lines], tables[3, lines]))

    def from_field(group, field):
        lanes = []
        for inner in range(STEP_PLANES):
            plane = group * STEP_PLANES + inner
            pos_x = ((rank_ref[0] * LOC + plane).astype(F32) + 0.5) / N - 0.5
            shift_x = (TURN * trap_strength) * pos_x * pos_x
            real = field[0, inner * N : (inner + 1) * N]
            imag = field[1, inner * N : (inner + 1) * N]
            turns = (base[...] + shift_x) + (TURN * coupling) * (real * real + imag * imag)
            rest = turns - jnp.round(turns)
            square = rest * rest
            sine = polynomial(SIN_C, square) * rest
            cosine = polynomial(COS_C, square)
            decay = jnp.exp2(turns * DECAY_LOG2 + AMP_LOG2)
            evo_real = decay * (1.0 - sine * sine)
            evo_imag = decay * (sine * cosine)
            moved_real = real * evo_real + imag * evo_imag + noise_ref[0, plane]
            moved_imag = imag * evo_real - real * evo_imag + noise_ref[1, plane]
            lanes.append(jnp.concatenate([moved_real, moved_imag], axis=1))
        value = dot3(split(jnp.concatenate(lanes, axis=0)), (tables[4], tables[5]))
        for inner in range(STEP_PLANES):
            rows = pl.ds(group * STEP_PLANES + inner, LOC, stride=LOC)
            both = value[inner * N : (inner + 1) * N]
            real, imag = column_transform((tables[6], tables[7]), both[:, :ZM], both[:, ZM:])
            for g in range(GRID):
                out_ref[g, 0, rows, :] = real[g * LOC : (g + 1) * LOC]
                out_ref[g, 1, rows, :] = imag[g * LOC : (g + 1) * LOC]

    @pl.when(step == 0)
    def _():
        for copy in table_copies[:2]:
            copy.start()
        noise_copy(0).start()
        table_copies[2].start()
        for later in range(1, groups):
            noise_copy(later).start()
        shape = (N, N)
        pos_y = (lax.broadcasted_iota(jnp.int32, shape, 0).astype(F32) + 0.5) / N - 0.5
        pos_z = (lax.broadcasted_iota(jnp.int32, shape, 1).astype(F32) + 0.5) / N - 0.5
        base[...] = TURN * (trap_strength * (pos_y * pos_y + pos_z * pos_z) - chem_potential)
        for copy in table_copies[:2]:
            copy.wait()
        to_field(0, first_field)
        table_copies[2].wait()

    def both_stages(source, target):
        noise_copy(step - 1).wait()
        from_field(step - 1, source)
        to_field(step, target)

    @pl.when((step > 0) & (step < groups) & (step % 2 == 1))
    def _():
        both_stages(first_field, second_field)

    @pl.when((step > 0) & (step < groups) & (step % 2 == 0))
    def _():
        both_stages(second_field, first_field)

    @pl.when(step == groups)
    def _():
        noise_copy(groups - 1).wait()
        from_field(groups - 1, (first_field, second_field)[(groups - 1) % 2])


def last_kernel(
    rank_ref, in_ref, mask_ref, table_ref, out_hbm, hist_ref, keep, field, occ_hi, occ_lo, sems
):
    keep[...] = select_tiles(mask_ref[...]).astype(F32).reshape(N * LOC, ZM)
    table = (table_ref[0], table_ref[1])
    lines = field.reshape(2, 2, N * LOC, ZM)
    low_lane = lax.broadcasted_iota(jnp.int32, (N, ZM), 1) < ZM // 2
    far = jnp.zeros((8, ZM), F32)
    for row in range(LOC):
        real, imag = column_transform(
            table, in_ref[:, 0, row].reshape(N, ZM), in_ref[:, 1, row].reshape(N, ZM)
        )
        rows = pl.ds(row, N, stride=LOC)
        mask = keep[rows, :]
        real = real * mask
        imag = imag * mask
        for half, value in enumerate((real, imag)):
            lines[half, 0, rows, :] = jnp.where(low_lane, value, 0.0)
            lines[half, 1, rows, :] = jnp.where(low_lane, 0.0, value)
        occupation = real * real + imag * imag
        far = far + jnp.sum(occupation[NEAR : N - NEAR].reshape(-1, 8, ZM), axis=0)
        near = jnp.concatenate([occupation[:NEAR], occupation[N - NEAR :]], axis=0)
        high, low = split(near)
        occ_hi[:, row * ZM : (row + 1) * ZM] = high
        occ_lo[:, row * ZM : (row + 1) * ZM] = low
    copies = [
        pltpu.make_async_copy(
            field.at[half, tile],
            out_hbm.at[0, half, :, :, pl.ds(tile * ZM, ZM)],
            sems.at[half, tile],
        )
        for half in range(2)
        for tile in range(2)
    ]
    for copy in copies:
        copy.start()

    shape = (LOC * ZM, SHELLS)
    place = lax.broadcasted_iota(jnp.int32, shape, 0)
    index_y = rank_ref[0] * LOC + (place >> 7)
    index_z = place & (ZM - 1)
    sig_y = jnp.where(index_y < N // 2, index_y, index_y - N)
    sig_z = jnp.where(index_z < ZM // 2, index_z, index_z - ZM)
    rest = jnp.minimum(sig_y * sig_y + sig_z * sig_z, 64 * (SHELLS - 1))
    gap = (rest - 64 * lax.broadcasted_iota(jnp.int32, shape, 1)).astype(F32)
    gap = jnp.clip(gap, -GAP_MAX, GAP_MAX).astype(BF16)
    count = 2 * NEAR
    shape = (count, SHELLS)
    index_x = lax.broadcasted_iota(jnp.int32, shape, 0)
    sig_x = jnp.where(index_x < NEAR, index_x, index_x - count)
    square_x = sig_x * sig_x
    residue = square_x & 63
    sums = jnp.zeros(shape, F32)
    one = jnp.ones((), BF16)
    zero = jnp.zeros((), BF16)
    for first in range(0, len(RESIDUES), 2):
        pair = RESIDUES[first : first + 2]
        hits = jnp.concatenate(
            [jnp.where(jnp.abs(gap + BF16(r - 31.5)) < BF16(32.0), one, zero) for r in pair], axis=1
        )
        found = dot(occ_hi[...], hits) + dot(occ_lo[...], hits)
        for place_of, r in enumerate(pair):
            sums = jnp.where(residue == r, found[:, place_of * SHELLS : (place_of + 1) * SHELLS], sums)
    moves = square_x >> 6
    bins = lax.broadcasted_iota(jnp.int32, shape, 1)
    beyond = moves >= SHELLS - 1
    over = jnp.where(beyond, sums, 0.0)
    sums = jnp.where(beyond, 0.0, sums)
    for bit in range(7):
        width = 1 << bit
        chosen = (moves & width) != 0
        past = chosen & (bins >= SHELLS - width)
        over = over + jnp.where(past, sums, 0.0)
        rolled = jnp.where(bins >= width, pltpu.roll(sums, width, 1), 0.0)
        sums = jnp.where(chosen, rolled, sums)
    total = jnp.sum(sums, axis=0, keepdims=True)
    extra = jnp.sum(over, axis=0, keepdims=True) + jnp.sum(far, axis=0, keepdims=True)
    extra = jnp.sum(extra, axis=1, keepdims=True)
    hist = total + jnp.where(bins[:1] == SHELLS - 1, extra, 0.0)
    hist_ref[...] = jnp.broadcast_to(hist.reshape(1, 1, SHELLS), (GRID, 1, SHELLS))
    for copy in copies:
        copy.wait()


def params(mib):
    return pltpu.CompilerParams(vmem_limit_bytes=mib * 1024 * 1024)


def whole(shape):
    return pl.BlockSpec(shape, lambda *_: (0,) * len(shape))


def exchange(value):
    return lax.all_to_all(value, "grid", split_axis=0, concat_axis=0, tiled=True)


def shards(psi_modes, noise, mask):
    inv_tall, fwd_tall, inv_z, fwd_z = (halves(table) for table in host_tables())
    tables = jnp.asarray(np.concatenate([inv_tall, inv_z, fwd_z, fwd_tall]))
    rank = lax.axis_index("grid").astype(jnp.int32).reshape(1)
    smem = pl.BlockSpec(memory_space=pltpu.SMEM)
    hbm = pl.BlockSpec(memory_space=pltpu.HBM)
    message = (GRID, 2, LOC, LOC, ZM)
    flat = (GRID, 2, LOC * LOC, ZM)
    sent = pl.pallas_call(
        first_kernel,
        out_shape=jax.ShapeDtypeStruct(message, F32),
        grid=(1,),
        in_specs=[hbm] * 3,
        out_specs=whole(message),
        scratch_shapes=[
            pltpu.VMEM((2, N, LOC, N), F32),
            pltpu.VMEM((N, LOC, N), jnp.int32),
            pltpu.VMEM((2, 2 * N, N), BF16),
            pltpu.VMEM((2, N * LOC, ZM), F32),
            pltpu.SemaphoreType.DMA((3, 4)),
        ],
        compiler_params=params(63),
        name="first",
    )(psi_modes, mask, tables)
    planes = exchange(sent).reshape(flat)
    sent = pl.pallas_call(
        plane_kernel,
        out_shape=jax.ShapeDtypeStruct(flat, F32),
        grid=(LOC // STEP_PLANES + 1,),
        in_specs=[
            smem,
            whole(flat),
            hbm,
            hbm,
        ],
        out_specs=whole(flat),
        scratch_shapes=[
            pltpu.VMEM((N, N), F32),
            pltpu.VMEM((2, LOC, N, N), F32),
            pltpu.VMEM(tables.shape, BF16),
            pltpu.VMEM((2, STEP_PLANES * N, N), F32),
            pltpu.VMEM((2, STEP_PLANES * N, N), F32),
            pltpu.SemaphoreType.DMA((LOC // STEP_PLANES + 3,)),
        ],
        compiler_params=params(PLANES_MIB),
        name="planes",
    )(rank, planes, noise, tables)
    rows_in = exchange(sent).reshape(message)
    psi_next, hist = pl.pallas_call(
        last_kernel,
        out_shape=(
            jax.ShapeDtypeStruct(psi_modes.shape, F32),
            jax.ShapeDtypeStruct((GRID, 1, SHELLS), F32),
        ),
        grid=(1,),
        in_specs=[smem, whole(message), whole((N, LOC, N)), pl.BlockSpec((2, 2 * N, N), lambda i: (3, 0, 0))],
        out_specs=(hbm, whole((GRID, 1, SHELLS))),
        scratch_shapes=[
            pltpu.VMEM((N * LOC, ZM), F32),
            pltpu.VMEM((2, 2, N, LOC, ZM), F32),
            pltpu.VMEM((2 * NEAR, LOC * ZM), BF16),
            pltpu.VMEM((2 * NEAR, LOC * ZM), BF16),
            pltpu.SemaphoreType.DMA((2, 2)),
        ],
        compiler_params=params(24),
        name="last",
    )(rank, rows_in, mask, tables)
    hist = jnp.sum(exchange(hist), axis=0)
    for bit in (1, 2):
        hist = hist + lax.ppermute(hist, "traj", [(t, t ^ bit) for t in range(TRAJ)])
    return psi_next, hist.reshape(SHELLS) * (SHELLS / (TRAJ * N * N * N))


def solution(mesh):
    placed = (
        P("traj", None, None, "grid", None),
        P("traj", None, "grid", None, None),
        P(None, "grid", None),
    )
    return jax.shard_map(
        shards,
        mesh=mesh,
        in_specs=placed,
        out_specs=(P("traj", None, None, "grid", None), P()),
        check_vma=False,
    )
```

time: 131 us -> 115 us (0.88)
  blocking collectives: 52.5 us -> 42.6 us
  Pallas kernels: 35.1 us -> 25.4 us
  starting transfers between devices: 8.55 us -> 13.1 us
  local copies, waits for them, and re-layouts: 4.21 us -> 0.01 us
  waiting for transfers between devices: 28.9 us -> 32.8 us
    all_to_all x2 -> x0, blocking collectives: 20.8 us -> none  [summed_over(): lax.all_to_all(copies, axis, split_axis=0, concat_axis=0, tiled=True)]
    all_to_all x1 -> x2, blocking collectives: 31.7 us -> 42.6 us  [exchange(): lax.all_to_all(value, 'grid', split_axis=0, concat_axis=0, tiled=True)]
    pallas_call x2, Pallas kernels: 26.7 us -> 20.7 us  [the longest x1 14.5 us: shards(): pl.pallas_call(plane_kernel, out_shape=jax.ShapeDtypeStruct(flat, F32), g...]
    ppermute x0 -> x2, starting transfers between devices: none -> 4.84 us  [shards(): lax.ppermute(hist, 'traj', [(t, t ^ bit) for t in range(TRAJ)])]
    ppermute x0 -> x2, waiting for transfers between devices: none -> 3.87 us  [shards(): lax.ppermute(hist, 'traj', [(t, t ^ bit) for t in range(TRAJ)])]
    pallas_call x1, Pallas kernels: 8.39 us -> 4.7 us  [shards(): pl.pallas_call(last_kernel, out_shape=(jax.ShapeDtypeStruct(psi_modes.sha...]
    unnamed x22 -> x4, local copies, waits for them, and re-layouts: 3.53 us -> 0.01 us
  transfers between devices with their start and end apart: 1 -> 3, of which waited for: 1 -> 3; matrix products, arithmetic and copies ran while one was open for 0% -> 0% of each run, Pallas kernels for 0% -> 0%
where the time goes in v1:
time: 115 us
  blocking collectives  42.6 us (37%)
  waiting for transfers between devices  32.8 us (29%)
  Pallas kernels  25.4 us (22%)
  starting transfers between devices  13.1 us (11%)
    all_to_all x2, blocking collectives, exchange(): lax.all_to_all(value, 'grid', split_axis=0, concat_axis=0, tiled=True)  42.6 us
    all_to_all x1, waiting for transfers between devices, exchange(): lax.all_to_all(value, 'grid', split_axis=0, concat_axis=0, tiled=True)  28.9 us
    pallas_call x1, Pallas kernels, shards(): pl.pallas_call(plane_kernel, out_shape=jax.ShapeDtypeStruct(flat, F32), g...  14.5 us
    all_to_all x1, starting transfers between devices, exchange(): lax.all_to_all(value, 'grid', split_axis=0, concat_axis=0, tiled=True)  8.29 us
    pallas_call x1, Pallas kernels, shards(): pl.pallas_call(first_kernel, out_shape=jax.ShapeDtypeStruct(message, F32)...  6.2 us
    ppermute x2, starting transfers between devices, shards(): lax.ppermute(hist, 'traj', [(t, t ^ bit) for t in range(TRAJ)])  4.84 us
    pallas_call x1, Pallas kernels, shards(): pl.pallas_call(last_kernel, out_shape=(jax.ShapeDtypeStruct(psi_modes.sha...  4.7 us
    ppermute x2, waiting for transfers between devices, shards(): lax.ppermute(hist, 'traj', [(t, t ^ bit) for t in range(TRAJ)])  3.87 us
  transfers between devices with their start and end apart: 3, of which 3 were waited for; matrix products, arithmetic and copies ran while one was open for 0% of the time, Pallas kernels for 0%

profile of v1, /device:TPU:0, one launch (start us, length us, event | category | flops | bytes accessed | tf_op | source)
XLA Modules:
  0.0 115.2 jit_solution(14028568870849890086)
XLA Ops:
  0.6 6.2 %first.1 = f32[32,2,8,8,128]{4,3,2,1,0:T(8,128)} custom-call(f32[1,2,256,8,256]{4,3,2,1,0:T(8,128)} %psi_hbm.1, s32[256,8,256]{2,1,0:T(8,128)} %mask_ref.1, bf16[8,512,256]{2,1,0:T(8,128)(2,1)} %constant.10.clone.table_hbm.tables_hbm.table_ref), custom_call_target="tpu_custom_call" | custom-call | tf_op jit(solution)/shard_map/first/pallas_call | solution.py:335
  6.8 8.3 %all-to-all-start = ((f32[32,2,8,8,128]{4,3,2,1,0:T(8,128)}), f32[32,2,8,8,128]{4,3,2,1,0:T(8,128)S(1)}, u32[]{:S(2)}, u32[]{:S(2)}) async-start(f32[32,2,8,8,128]{4,3,2,1,0:T(8,128)} %first.1), calls=%async_computation | async-start | bytes 4194304 | tf_op jit(solution)/shard_map/all_to_all | solution.py:324
  15.1 28.9 %all-to-all-done = f32[32,2,8,8,128]{4,3,2,1,0:T(8,128)S(1)} async-done(((f32[32,2,8,8,128]{4,3,2,1,0:T(8,128)}), f32[32,2,8,8,128]{4,3,2,1,0:T(8,128)S(1)}, u32[]{:S(2)}, u32[]{:S(2)}) %all-to-all-start) | async-done | bytes 2097184 | tf_op jit(solution)/shard_map/all_to_all | solution.py:324
  44.1 14.5 %planes.1 = f32[32,2,64,128]{3,2,1,0:T(8,128)S(1)} custom-call(s32[1]{0:T(128)} %bitcast.rank_ref, f32[32,2,64,128]{3,2,1,0:T(8,128)S(1)} %bitcast.8, f32[1,2,8,256,256]{4,3,2,1,0:T(8,128)} %noise_hbm.1, bf16[8,512,256]{2,1,0:T(8,128)(2,1)} %constant.10.clone.table_hbm.tables_hbm.table_ref), custom_call_target="tpu_custom_call" | custom-call | tf_op jit(solution)/shard_map/planes/pallas_call | solution.py:352
  58.6 0.0 copy-start
  58.6 0.0 copy-start.1
  58.6 31.3 %all_to_all.15 = f32[32,2,64,128]{3,2,1,0:T(8,128)S(1)} all-to-all(f32[32,2,64,128]{3,2,1,0:T(8,128)S(1)} %planes.1), channel_id=1, replica_groups=mesh['traj'=4,'grid'=32] {'grid'}, dimensions={0} | all-to-all | bytes 4194304 | tf_op jit(solution)/shard_map/all_to_all | solution.py:324
  89.9 0.0 copy-done
  89.9 0.0 copy-done.1
  89.9 4.7 %last.1 = (f32[1,2,256,8,256]{4,3,2,1,0:T(8,128)}, f32[32,1,128]{2,1,0:T(1,128)S(1)}) custom-call(s32[1]{0:T(128)} %bitcast.rank_ref, f32[32,2,8,8,128]{4,3,2,1,0:T(8,128)S(1)} %bitcast.7, s32[256,8,256]{2,1,0:T(8,128)S(1)} %copy-done.1, bf16[8,512,256]{2,1,0:T(8,128)(2,1)S(1)} %copy-done), custom_call_target="tpu_custom_call" | custom-call | tf_op jit(solution)/shard_map/last/pallas_call | solution.py:375
  94.7 11.2 %all_to_all.16 = f32[32,1,128]{2,1,0:T(1,128)S(1)} all-to-all(f32[32,1,128]{2,1,0:T(1,128)S(1)} %get-tuple-element.5), channel_id=1, replica_groups=mesh['traj'=4,'grid'=32] {'grid'}, dimensions={0} | all-to-all | bytes 32768 | tf_op jit(solution)/shard_map/all_to_all | solution.py:324
  105.9 0.1 reduce_sum.11
  106.0 1.6 %collective-permute-start = (f32[1,128]{1,0:T(1,128)S(1)}, f32[1,128]{1,0:T(1,128)S(1)}, u32[]{:S(2)}, u32[]{:S(2)}) collective-permute-start(f32[1,128]{1,0:T(1,128)S(1)} %bitcast.9), channel_id=1, source_target_pairs={{0,32},{32,0},{64,96},{96,64},{1,33},{33,1},{65,97},{97,65},{2,34}... | collective-permute-start | bytes 1544 | tf_op jit(solution)/shard_map/ppermute | solution.py:396
  107.6 2.0 %collective-permute-done = f32[1,128]{1,0:T(1,128)S(1)} collective-permute-done((f32[1,128]{1,0:T(1,128)S(1)}, f32[1,128]{1,0:T(1,128)S(1)}, u32[]{:S(2)}, u32[]{:S(2)}) %collective-permute-start) | collective-permute-done | bytes 544 | tf_op jit(solution)/shard_map/ppermute | solution.py:396
  109.6 3.2 %collective-permute-start.1 = (f32[1,128]{1,0:T(1,128)S(1)}, f32[1,128]{1,0:T(1,128)S(1)}, u32[]{:S(2)}, u32[]{:S(2)}) collective-permute-start(f32[1,128]{1,0:T(1,128)S(1)} %bitcast_add_fusion), channel_id=1, source_target_pairs={{0,64},{32,96},{64,0},{96,32},{1,65},{33,97},{65,1},{97,33},{2,66}... | collective-permute-start | bytes 1544 | tf_op jit(solution)/shard_map/ppermute | solution.py:396
  112.8 1.9 %collective-permute-done.1 = f32[1,128]{1,0:T(1,128)S(1)} collective-permute-done((f32[1,128]{1,0:T(1,128)S(1)}, f32[1,128]{1,0:T(1,128)S(1)}, u32[]{:S(2)}, u32[]{:S(2)}) %collective-permute-start.1) | collective-permute-done | bytes 544 | tf_op jit(solution)/shard_map/ppermute | solution.py:396
  114.7 0.5 multiply_bitcast_fusion
  (1 shorter events, 0.0 us)
Async XLA Ops:
  6.8 37.2 %all-to-all-start = ((f32[32,2,8,8,128]{4,3,2,1,0:T(8,128)}), f32[32,2,8,8,128]{4,3,2,1,0:T(8,128)S(1)}, u32[]{:S(2)}, u32[]{:S(2)}) async-start(f32[32,2,8,8,128]{4,3,2,1,0:T(8,128)} %first.1), calls=%async_computation | async-start | bytes 4194304 | tf_op jit(solution)/shard_map/all_to_all | solution.py:324
  58.6 31.3 %copy-start = (bf16[8,512,256]{2,1,0:T(8,128)(2,1)S(1)}, bf16[8,512,256]{2,1,0:T(8,128)(2,1)}, u32[]{:S(2)}) copy-start(bf16[8,512,256]{2,1,0:T(8,128)(2,1)} %constant.10.clone.table_hbm.tables_hbm.table_ref) | copy-start | bytes 6291460
  58.6 31.3 %copy-start.1 = (s32[256,8,256]{2,1,0:T(8,128)S(1)}, s32[256,8,256]{2,1,0:T(8,128)}, u32[]{:S(2)}) copy-start(s32[256,8,256]{2,1,0:T(8,128)} %mask_ref.1) | copy-start | bytes 6291460
  106.0 3.6 %collective-permute-start = (f32[1,128]{1,0:T(1,128)S(1)}, f32[1,128]{1,0:T(1,128)S(1)}, u32[]{:S(2)}, u32[]{:S(2)}) collective-permute-start(f32[1,128]{1,0:T(1,128)S(1)} %bitcast.9), channel_id=1, source_target_pairs={{0,32},{32,0},{64,96},{96,64},{1,33},{33,1},{65,97},{97,65},{2,34}... | collective-permute-start | bytes 1544 | tf_op jit(solution)/shard_map/ppermute | solution.py:396
  109.6 5.1 %collective-permute-start.1 = (f32[1,128]{1,0:T(1,128)S(1)}, f32[1,128]{1,0:T(1,128)S(1)}, u32[]{:S(2)}, u32[]{:S(2)}) collective-permute-start(f32[1,128]{1,0:T(1,128)S(1)} %bitcast_add_fusion), channel_id=1, source_target_pairs={{0,64},{32,96},{64,0},{96,32},{1,65},{33,97},{65,1},{97,33},{2,66}... | collective-permute-start | bytes 1544 | tf_op jit(solution)/shard_map/ppermute | solution.py:396

commit v2 on v1

--- a/solution.py
+++ b/solution.py
@@ -13,7 +13,7 @@
 ZM = N // 2
 TRAJ = 4
 PLANES_MIB = 48
-STEP_PLANES = 2
+STEP_PLANES = 4
 
 time_step = 1.0
 damping = 0.05
@@ -99,46 +99,61 @@
     return value
 
 
-def first_kernel(psi_hbm, mask_hbm, table_hbm, out_ref, psi, mask, table_ref, field, sems):
+def first_kernel(psi_hbm, mask_hbm, table_hbm, out_hbm, psi, mask, table_ref, keep, field, partial, out, sems):
     pieces = 4
-    rows = N // pieces
-    copies = []
+    count = N // pieces
+    copies = [[], [], []]
     for piece in range(pieces):
-        part = pl.ds(piece * rows, rows)
-        copies.append(
-            (
-                pltpu.make_async_copy(psi_hbm.at[0, :, part], psi.at[:, part], sems.at[0, piece]),
-                pltpu.make_async_copy(mask_hbm.at[part], mask.at[part], sems.at[1, piece]),
+        part = pl.ds(piece * count, count)
+        copies[0].append(pltpu.make_async_copy(mask_hbm.at[part], mask.at[part], sems.at[0, piece]))
+        for half in range(2):
+            copies[1 + half].append(
+                pltpu.make_async_copy(psi_hbm.at[0, half, part], psi.at[half, part], sems.at[1 + half, piece])
             )
-        )
-    tables = [pltpu.make_async_copy(table_hbm.at[pl.ds(0, 2)], table_ref, sems.at[2, 0])]
-    for pair in copies:
+    table_copy = pltpu.make_async_copy(table_hbm.at[pl.ds(0, 2)], table_ref, sems.at[3, 0])
+    for pair in zip(*copies[:2]):
         for copy in pair:
             copy.start()
-    for copy in tables:
+    table_copy.start()
+    for copy in copies[2]:
         copy.start()
-    for piece, pair in enumerate(copies):
-        for copy in pair:
-            copy.wait()
-        part = slice(piece * rows, (piece + 1) * rows)
-        keep = select_tiles(mask[part]).astype(F32)
-        for half in range(2):
-            field[half, piece * rows * LOC : (piece + 1) * rows * LOC] = (
-                select_tiles(psi[half, part]) * keep
-            ).reshape(rows * LOC, ZM)
-    for copy in tables:
+    table = None
+    sent = []
+    for half in range(2):
+        for piece in range(pieces):
+            part = slice(piece * count, (piece + 1) * count)
+            lines = slice(piece * count * LOC, (piece + 1) * count * LOC)
+            if half == 0:
+                copies[0][piece].wait()
+                keep[lines] = select_tiles(mask[part]).astype(F32).reshape(count * LOC, ZM)
+            copies[1 + half][piece].wait()
+            field[half, lines] = select_tiles(psi[half, part]).reshape(count * LOC, ZM) * keep[lines]
+        if half == 0:
+            table_copy.wait()
+            table = (table_ref[0], table_ref[1])
+        for pair in range(LOC // 2):
+            value = jnp.concatenate(
+                [field[half, pl.ds(2 * pair + k, N, stride=LOC), :] for k in range(2)], axis=1
+            )
+            value = dot3(table, split(value))
+            if half == 0:
+                partial[pair] = value
+            else:
+                real = partial[pair, :N] - value[N:]
+                imag = partial[pair, N:] + value[:N]
+                for k in range(2):
+                    lanes = slice(k * ZM, (k + 1) * ZM)
+                    out[:, 0, 2 * pair + k] = real[:, lanes].reshape(GRID, LOC, ZM)
+                    out[:, 1, 2 * pair + k] = imag[:, lanes].reshape(GRID, LOC, ZM)
+                rows = pl.ds(2 * pair, 2)
+                sent.append(pltpu.make_async_copy(out.at[:, :, rows], out_hbm.at[:, :, rows], sems.at[4, pair]))
+                sent[-1].start()
+    for copy in sent:
         copy.wait()
-    table = (table_ref[0], table_ref[1])
-    for row in range(LOC):
-        real, imag = column_transform(
-            table, field[0, pl.ds(row, N, stride=LOC), :], field[1, pl.ds(row, N, stride=LOC), :]
-        )
-        out_ref[:, 0, row] = real.reshape(GRID, LOC, ZM)
-        out_ref[:, 1, row] = imag.reshape(GRID, LOC, ZM)
 
 
 def plane_kernel(
-    rank_ref, in_ref, noise_hbm, tables_hbm, out_ref, base, noise_ref, tables, first_field, second_field, sems
+    rank_ref, in_ref, noise_hbm, tables_hbm, out_ref, base, noise_ref, tables, sems
 ):
     step = pl.program_id(0)
     groups = LOC // STEP_PLANES
@@ -151,7 +166,7 @@
         planes = pl.ds(group * STEP_PLANES, STEP_PLANES)
         return pltpu.make_async_copy(noise_hbm.at[0, :, planes], noise_ref.at[:, planes], sems.at[group])
 
-    def to_field(group, field):
+    def to_field(group):
         lanes = []
         for inner in range(STEP_PLANES):
             rows = pl.ds(group * STEP_PLANES + inner, LOC, stride=LOC)
@@ -160,9 +175,8 @@
             real, imag = column_transform((tables[0], tables[1]), real, imag)
             lanes.append(jnp.concatenate([real, imag], axis=1))
         value = split(jnp.concatenate(lanes, axis=0))
-        for part in range(2):
-            lines = pl.ds(part * N, N)
-            field[part] = dot3(value, (tables[2, lines], tables[3, lines]))
+        parts = (pl.ds(0, N), pl.ds(N, N))
+        return [dot3(value, (tables[2, lines], tables[3, lines])) for lines in parts]
 
     def from_field(group, field):
         lanes = []
@@ -170,8 +184,8 @@
             plane = group * STEP_PLANES + inner
             pos_x = ((rank_ref[0] * LOC + plane).astype(F32) + 0.5) / N - 0.5
             shift_x = (TURN * trap_strength) * pos_x * pos_x
-            real = field[0, inner * N : (inner + 1) * N]
-            imag = field[1, inner * N : (inner + 1) * N]
+            real = field[0][inner * N : (inner + 1) * N]
+            imag = field[1][inner * N : (inner + 1) * N]
             turns = (base[...] + shift_x) + (TURN * coupling) * (real * real + imag * imag)
             rest = turns - jnp.round(turns)
             square = rest * rest
@@ -206,30 +220,19 @@
         base[...] = TURN * (trap_strength * (pos_y * pos_y + pos_z * pos_z) - chem_potential)
         for copy in table_copies[:2]:
             copy.wait()
-        to_field(0, first_field)
+
+    field = to_field(step)
+    noise_copy(step).wait()
+
+    @pl.when(step == 0)
+    def _():
         table_copies[2].wait()
 
-    def both_stages(source, target):
-        noise_copy(step - 1).wait()
-        from_field(step - 1, source)
-        to_field(step, target)
-
-    @pl.when((step > 0) & (step < groups) & (step % 2 == 1))
-    def _():
-        both_stages(first_field, second_field)
-
-    @pl.when((step > 0) & (step < groups) & (step % 2 == 0))
-    def _():
-        both_stages(second_field, first_field)
-
-    @pl.when(step == groups)
-    def _():
-        noise_copy(groups - 1).wait()
-        from_field(groups - 1, (first_field, second_field)[(groups - 1) % 2])
+    from_field(step, field)
 
 
 def last_kernel(
-    rank_ref, in_ref, mask_ref, table_ref, out_hbm, hist_ref, keep, field, occ_hi, occ_lo, sems
+    rank_ref, in_ref, mask_ref, table_ref, out_hbm, hist_ref, keep, field, occ, sems
 ):
     keep[...] = select_tiles(mask_ref[...]).astype(F32).reshape(N * LOC, ZM)
     table = (table_ref[0], table_ref[1])
@@ -251,8 +254,8 @@
         far = far + jnp.sum(occupation[NEAR : N - NEAR].reshape(-1, 8, ZM), axis=0)
         near = jnp.concatenate([occupation[:NEAR], occupation[N - NEAR :]], axis=0)
         high, low = split(near)
-        occ_hi[:, row * ZM : (row + 1) * ZM] = high
-        occ_lo[:, row * ZM : (row + 1) * ZM] = low
+        occ[: 2 * NEAR, row * ZM : (row + 1) * ZM] = high
+        occ[2 * NEAR :, row * ZM : (row + 1) * ZM] = low
     copies = [
         pltpu.make_async_copy(
             field.at[half, tile],
@@ -288,7 +291,8 @@
         hits = jnp.concatenate(
             [jnp.where(jnp.abs(gap + BF16(r - 31.5)) < BF16(32.0), one, zero) for r in pair], axis=1
         )
-        found = dot(occ_hi[...], hits) + dot(occ_lo[...], hits)
+        found = dot(occ[...], hits)
+        found = found[:count] + found[count:]
         for place_of, r in enumerate(pair):
             sums = jnp.where(residue == r, found[:, place_of * SHELLS : (place_of + 1) * SHELLS], sums)
     moves = square_x >> 6
@@ -337,13 +341,16 @@
         out_shape=jax.ShapeDtypeStruct(message, F32),
         grid=(1,),
         in_specs=[hbm] * 3,
-        out_specs=whole(message),
+        out_specs=hbm,
         scratch_shapes=[
             pltpu.VMEM((2, N, LOC, N), F32),
             pltpu.VMEM((N, LOC, N), jnp.int32),
             pltpu.VMEM((2, 2 * N, N), BF16),
+            pltpu.VMEM((N * LOC, ZM), F32),
             pltpu.VMEM((2, N * LOC, ZM), F32),
-            pltpu.SemaphoreType.DMA((3, 4)),
+            pltpu.VMEM((LOC // 2, 2 * N, 2 * ZM), F32),
+            pltpu.VMEM(message, F32),
+            pltpu.SemaphoreType.DMA((5, 4)),
         ],
         compiler_params=params(63),
         name="first",
@@ -352,7 +359,7 @@
     sent = pl.pallas_call(
         plane_kernel,
         out_shape=jax.ShapeDtypeStruct(flat, F32),
-        grid=(LOC // STEP_PLANES + 1,),
+        grid=(LOC // STEP_PLANES,),
         in_specs=[
             smem,
             whole(flat),
@@ -364,8 +371,6 @@
             pltpu.VMEM((N, N), F32),
             pltpu.VMEM((2, LOC, N, N), F32),
             pltpu.VMEM(tables.shape, BF16),
-            pltpu.VMEM((2, STEP_PLANES * N, N), F32),
-            pltpu.VMEM((2, STEP_PLANES * N, N), F32),
             pltpu.SemaphoreType.DMA((LOC // STEP_PLANES + 3,)),
         ],
         compiler_params=params(PLANES_MIB),
@@ -384,8 +389,7 @@
         scratch_shapes=[
             pltpu.VMEM((N * LOC, ZM), F32),
             pltpu.VMEM((2, 2, N, LOC, ZM), F32),
-            pltpu.VMEM((2 * NEAR, LOC * ZM), BF16),
-            pltpu.VMEM((2 * NEAR, LOC * ZM), BF16),
+            pltpu.VMEM((4 * NEAR, LOC * ZM), BF16),
             pltpu.SemaphoreType.DMA((2, 2)),
         ],
         compiler_params=params(24),

time: 115 us -> 114 us (level)
  Pallas kernels: 25.4 us -> 24.1 us
where the time goes in v2:
time: 114 us
  blocking collectives  42.5 us (37%)
  waiting for transfers between devices  32.8 us (29%)
  Pallas kernels  24.1 us (21%)
  starting transfers between devices  13.1 us (11%)
    all_to_all x2, blocking collectives, exchange(): lax.all_to_all(value, 'grid', split_axis=0, concat_axis=0, tiled=True)  42.5 us
    all_to_all x1, waiting for transfers between devices, exchange(): lax.all_to_all(value, 'grid', split_axis=0, concat_axis=0, tiled=True)  28.9 us
    pallas_call x1, Pallas kernels, shards(): pl.pallas_call(plane_kernel, out_shape=jax.ShapeDtypeStruct(flat, F32), g...  13.8 us
    all_to_all x1, starting transfers between devices, exchange(): lax.all_to_all(value, 'grid', split_axis=0, concat_axis=0, tiled=True)  8.29 us
    pallas_call x1, Pallas kernels, shards(): pl.pallas_call(first_kernel, out_shape=jax.ShapeDtypeStruct(message, F32)...  5.71 us
    ppermute x2, starting transfers between devices, shards(): lax.ppermute(hist, 'traj', [(t, t ^ bit) for t in range(TRAJ)])  4.85 us
    pallas_call x1, Pallas kernels, shards(): pl.pallas_call(last_kernel, out_shape=(jax.ShapeDtypeStruct(psi_modes.sha...  4.66 us
    ppermute x2, waiting for transfers between devices, shards(): lax.ppermute(hist, 'traj', [(t, t ^ bit) for t in range(TRAJ)])  3.86 us
  transfers between devices with their start and end apart: 3, of which 3 were waited for; matrix products, arithmetic and copies ran while one was open for 0% of the time, Pallas kernels for 0%

profile of v2, /device:TPU:0, one launch (start us, length us, event | category | flops | bytes accessed | tf_op | source)
XLA Modules:
  0.0 113.9 jit_solution(18284892166988316989)
XLA Ops:
  0.6 5.7 %first.1 = f32[32,2,8,8,128]{4,3,2,1,0:T(8,128)} custom-call(f32[1,2,256,8,256]{4,3,2,1,0:T(8,128)} %psi_hbm.1, s32[256,8,256]{2,1,0:T(8,128)} %mask_ref.1, bf16[8,512,256]{2,1,0:T(8,128)(2,1)} %constant.10.clone.table_hbm.tables_hbm.table_ref), custom_call_target="tpu_custom_call" | custom-call | tf_op jit(solution)/shard_map/first/pallas_call | solution.py:339
  6.3 8.3 %all-to-all-start = ((f32[32,2,8,8,128]{4,3,2,1,0:T(8,128)}), f32[32,2,8,8,128]{4,3,2,1,0:T(8,128)S(1)}, u32[]{:S(2)}, u32[]{:S(2)}) async-start(f32[32,2,8,8,128]{4,3,2,1,0:T(8,128)} %first.1), calls=%async_computation | async-start | bytes 4194304 | tf_op jit(solution)/shard_map/all_to_all | solution.py:328
  14.6 28.9 %all-to-all-done = f32[32,2,8,8,128]{4,3,2,1,0:T(8,128)S(1)} async-done(((f32[32,2,8,8,128]{4,3,2,1,0:T(8,128)}), f32[32,2,8,8,128]{4,3,2,1,0:T(8,128)S(1)}, u32[]{:S(2)}, u32[]{:S(2)}) %all-to-all-start) | async-done | bytes 2097184 | tf_op jit(solution)/shard_map/all_to_all | solution.py:328
  43.6 13.8 %planes.1 = f32[32,2,64,128]{3,2,1,0:T(8,128)S(1)} custom-call(s32[1]{0:T(128)} %bitcast.rank_ref, f32[32,2,64,128]{3,2,1,0:T(8,128)S(1)} %bitcast.8, f32[1,2,8,256,256]{4,3,2,1,0:T(8,128)} %noise_hbm.1, bf16[8,512,256]{2,1,0:T(8,128)(2,1)} %constant.10.clone.table_hbm.tables_hbm.table_ref), custom_call_target="tpu_custom_call" | custom-call | tf_op jit(solution)/shard_map/planes/pallas_call | solution.py:359
  57.4 0.0 copy-start
  57.4 0.0 copy-start.1
  57.4 31.3 %all_to_all.15 = f32[32,2,64,128]{3,2,1,0:T(8,128)S(1)} all-to-all(f32[32,2,64,128]{3,2,1,0:T(8,128)S(1)} %planes.1), channel_id=1, replica_groups=mesh['traj'=4,'grid'=32] {'grid'}, dimensions={0} | all-to-all | bytes 4194304 | tf_op jit(solution)/shard_map/all_to_all | solution.py:328
  88.7 0.0 copy-done
  88.7 0.0 copy-done.1
  88.7 4.7 %last.1 = (f32[1,2,256,8,256]{4,3,2,1,0:T(8,128)}, f32[32,1,128]{2,1,0:T(1,128)S(1)}) custom-call(s32[1]{0:T(128)} %bitcast.rank_ref, f32[32,2,8,8,128]{4,3,2,1,0:T(8,128)S(1)} %bitcast.7, s32[256,8,256]{2,1,0:T(8,128)S(1)} %copy-done.1, bf16[8,512,256]{2,1,0:T(8,128)(2,1)S(1)} %copy-done), custom_call_target="tpu_custom_call" | custom-call | tf_op jit(solution)/shard_map/last/pallas_call | solution.py:380
  93.4 11.2 %all_to_all.16 = f32[32,1,128]{2,1,0:T(1,128)S(1)} all-to-all(f32[32,1,128]{2,1,0:T(1,128)S(1)} %get-tuple-element.5), channel_id=1, replica_groups=mesh['traj'=4,'grid'=32] {'grid'}, dimensions={0} | all-to-all | bytes 32768 | tf_op jit(solution)/shard_map/all_to_all | solution.py:328
  104.6 0.1 reduce_sum.11
  104.6 1.7 %collective-permute-start = (f32[1,128]{1,0:T(1,128)S(1)}, f32[1,128]{1,0:T(1,128)S(1)}, u32[]{:S(2)}, u32[]{:S(2)}) collective-permute-start(f32[1,128]{1,0:T(1,128)S(1)} %bitcast.9), channel_id=1, source_target_pairs={{0,32},{32,0},{64,96},{96,64},{1,33},{33,1},{65,97},{97,65},{2,34}... | collective-permute-start | bytes 1544 | tf_op jit(solution)/shard_map/ppermute | solution.py:400
  106.3 2.0 %collective-permute-done = f32[1,128]{1,0:T(1,128)S(1)} collective-permute-done((f32[1,128]{1,0:T(1,128)S(1)}, f32[1,128]{1,0:T(1,128)S(1)}, u32[]{:S(2)}, u32[]{:S(2)}) %collective-permute-start) | collective-permute-done | bytes 544 | tf_op jit(solution)/shard_map/ppermute | solution.py:400
  108.3 3.2 %collective-permute-start.1 = (f32[1,128]{1,0:T(1,128)S(1)}, f32[1,128]{1,0:T(1,128)S(1)}, u32[]{:S(2)}, u32[]{:S(2)}) collective-permute-start(f32[1,128]{1,0:T(1,128)S(1)} %bitcast_add_fusion), channel_id=1, source_target_pairs={{0,64},{32,96},{64,0},{96,32},{1,65},{33,97},{65,1},{97,33},{2,66}... | collective-permute-start | bytes 1544 | tf_op jit(solution)/shard_map/ppermute | solution.py:400
  111.5 1.9 %collective-permute-done.1 = f32[1,128]{1,0:T(1,128)S(1)} collective-permute-done((f32[1,128]{1,0:T(1,128)S(1)}, f32[1,128]{1,0:T(1,128)S(1)}, u32[]{:S(2)}, u32[]{:S(2)}) %collective-permute-start.1) | collective-permute-done | bytes 544 | tf_op jit(solution)/shard_map/ppermute | solution.py:400
  113.4 0.5 multiply_bitcast_fusion
  (1 shorter events, 0.0 us)
Async XLA Ops:
  6.3 37.2 %all-to-all-start = ((f32[32,2,8,8,128]{4,3,2,1,0:T(8,128)}), f32[32,2,8,8,128]{4,3,2,1,0:T(8,128)S(1)}, u32[]{:S(2)}, u32[]{:S(2)}) async-start(f32[32,2,8,8,128]{4,3,2,1,0:T(8,128)} %first.1), calls=%async_computation | async-start | bytes 4194304 | tf_op jit(solution)/shard_map/all_to_all | solution.py:328
  57.4 31.3 %copy-start = (bf16[8,512,256]{2,1,0:T(8,128)(2,1)S(1)}, bf16[8,512,256]{2,1,0:T(8,128)(2,1)}, u32[]{:S(2)}) copy-start(bf16[8,512,256]{2,1,0:T(8,128)(2,1)} %constant.10.clone.table_hbm.tables_hbm.table_ref) | copy-start | bytes 6291460
  57.4 31.3 %copy-start.1 = (s32[256,8,256]{2,1,0:T(8,128)S(1)}, s32[256,8,256]{2,1,0:T(8,128)}, u32[]{:S(2)}) copy-start(s32[256,8,256]{2,1,0:T(8,128)} %mask_ref.1) | copy-start | bytes 6291460
  104.6 3.6 %collective-permute-start = (f32[1,128]{1,0:T(1,128)S(1)}, f32[1,128]{1,0:T(1,128)S(1)}, u32[]{:S(2)}, u32[]{:S(2)}) collective-permute-start(f32[1,128]{1,0:T(1,128)S(1)} %bitcast.9), channel_id=1, source_target_pairs={{0,32},{32,0},{64,96},{96,64},{1,33},{33,1},{65,97},{97,65},{2,34}... | collective-permute-start | bytes 1544 | tf_op jit(solution)/shard_map/ppermute | solution.py:400
  108.3 5.1 %collective-permute-start.1 = (f32[1,128]{1,0:T(1,128)S(1)}, f32[1,128]{1,0:T(1,128)S(1)}, u32[]{:S(2)}, u32[]{:S(2)}) collective-permute-start(f32[1,128]{1,0:T(1,128)S(1)} %bitcast_add_fusion), channel_id=1, source_target_pairs={{0,64},{32,96},{64,0},{96,32},{1,65},{33,97},{65,1},{97,33},{2,66}... | collective-permute-start | bytes 1544 | tf_op jit(solution)/shard_map/ppermute | solution.py:400

commit v3 on v2

--- a/solution.py
+++ b/solution.py
@@ -232,48 +232,80 @@
 
 
 def last_kernel(
-    rank_ref, in_ref, mask_ref, table_ref, out_hbm, hist_ref, keep, field, occ, sems
+    rank_ref, in_ref, mask_ref, table_ref, out_hbm, hist_ref, keep, field, occ, halves_ref, sems
 ):
     keep[...] = select_tiles(mask_ref[...]).astype(F32).reshape(N * LOC, ZM)
-    table = (table_ref[0], table_ref[1])
     lines = field.reshape(2, 2, N * LOC, ZM)
-    low_lane = lax.broadcasted_iota(jnp.int32, (N, ZM), 1) < ZM // 2
+    half_rows = N // 2
+    low_lane = lax.broadcasted_iota(jnp.int32, (half_rows, ZM), 1) < ZM // 2
     far = jnp.zeros((8, ZM), F32)
-    for row in range(LOC):
-        real, imag = column_transform(
-            table, in_ref[:, 0, row].reshape(N, ZM), in_ref[:, 1, row].reshape(N, ZM)
+    mirror = lax.broadcasted_iota(jnp.int32, (NEAR, ZM), 1)
+    low_near = mirror < ZM // 2
+    mirror = jnp.where((mirror & (ZM // 2 - 1)) == 0, ZM // 2 - mirror, ZM - mirror)
+    copies = []
+    for upper in range(2):
+        first = upper * half_rows
+        table = tuple(
+            jnp.concatenate(
+                [table_ref[k, first : first + half_rows], table_ref[k, N + first : N + first + half_rows]], axis=0
+            )
+            for k in range(2)
         )
-        rows = pl.ds(row, N, stride=LOC)
-        mask = keep[rows, :]
-        real = real * mask
-        imag = imag * mask
-        for half, value in enumerate((real, imag)):
-            lines[half, 0, rows, :] = jnp.where(low_lane, value, 0.0)
-            lines[half, 1, rows, :] = jnp.where(low_lane, 0.0, value)
-        occupation = real * real + imag * imag
-        far = far + jnp.sum(occupation[NEAR : N - NEAR].reshape(-1, 8, ZM), axis=0)
-        near = jnp.concatenate([occupation[:NEAR], occupation[N - NEAR :]], axis=0)
-        high, low = split(near)
-        occ[: 2 * NEAR, row * ZM : (row + 1) * ZM] = high
-        occ[2 * NEAR :, row * ZM : (row + 1) * ZM] = low
-    copies = [
-        pltpu.make_async_copy(
-            field.at[half, tile],
-            out_hbm.at[0, half, :, :, pl.ds(tile * ZM, ZM)],
-            sems.at[half, tile],
-        )
-        for half in range(2)
-        for tile in range(2)
-    ]
-    for copy in copies:
-        copy.start()
-
-    shape = (LOC * ZM, SHELLS)
+        even = None
+        for row in range(LOC):
+            if upper == 0:
+                value = jnp.concatenate(
+                    [in_ref[:, 0, row].reshape(N, ZM), in_ref[:, 1, row].reshape(N, ZM)], axis=1
+                )
+                held = split(value)
+                halves_ref[row, 0] = held[0]
+                halves_ref[row, 1] = held[1]
+            else:
+                held = halves_ref[row, 0], halves_ref[row, 1]
+            both = dot3(table, held)
+            real = both[:half_rows, :ZM] - both[half_rows:, ZM:]
+            imag = both[:half_rows, ZM:] + both[half_rows:, :ZM]
+            rows = pl.ds(first * LOC + row, half_rows, stride=LOC)
+            mask = keep[rows, :]
+            real = real * mask
+            imag = imag * mask
+            for half, value in enumerate((real, imag)):
+                lines[half, 0, rows, :] = jnp.where(low_lane, value, 0.0)
+                lines[half, 1, rows, :] = jnp.where(low_lane, 0.0, value)
+            occupation = real * real + imag * imag
+            if upper == 0:
+                near, rest = occupation[:NEAR], occupation[NEAR:]
+            else:
+                rest, near = occupation[: half_rows - NEAR], occupation[half_rows - NEAR :]
+            far = far + jnp.sum(rest.reshape(-1, 8, ZM), axis=0)
+            if row % 2 == 0:
+                even = near
+                continue
+            folded = jnp.where(low_near, even, near) + jnp.take_along_axis(
+                jnp.where(low_near, near, even), mirror, axis=1, mode="promise_in_bounds"
+            )
+            high, low = split(folded)
+            lanes = slice(row // 2 * ZM, (row // 2 + 1) * ZM)
+            occ[upper * NEAR : (upper + 1) * NEAR, lanes] = high
+            occ[(2 + upper) * NEAR : (3 + upper) * NEAR, lanes] = low
+        part = pl.ds(first, half_rows)
+        for half in range(2):
+            for tile in range(2):
+                copies.append(
+                    pltpu.make_async_copy(
+                        field.at[half, tile, part],
+                        out_hbm.at[0, half, part, :, pl.ds(tile * ZM, ZM)],
+                        sems.at[half, 2 * upper + tile],
+                    )
+                )
+                copies[-1].start()
+
+    shape = (LOC * ZM // 2, SHELLS)
     place = lax.broadcasted_iota(jnp.int32, shape, 0)
-    index_y = rank_ref[0] * LOC + (place >> 7)
-    index_z = place & (ZM - 1)
+    lane = place & (ZM - 1)
+    index_y = rank_ref[0] * LOC + 2 * (place >> 7) + (lane >> 6)
     sig_y = jnp.where(index_y < N // 2, index_y, index_y - N)
-    sig_z = jnp.where(index_z < ZM // 2, index_z, index_z - ZM)
+    sig_z = jnp.where(lane < ZM // 2, lane, (ZM - lane) & (ZM // 2 - 1))
     rest = jnp.minimum(sig_y * sig_y + sig_z * sig_z, 64 * (SHELLS - 1))
     gap = (rest - 64 * lax.broadcasted_iota(jnp.int32, shape, 1)).astype(F32)
     gap = jnp.clip(gap, -GAP_MAX, GAP_MAX).astype(BF16)
@@ -389,8 +421,9 @@
         scratch_shapes=[
             pltpu.VMEM((N * LOC, ZM), F32),
             pltpu.VMEM((2, 2, N, LOC, ZM), F32),
-            pltpu.VMEM((4 * NEAR, LOC * ZM), BF16),
-            pltpu.SemaphoreType.DMA((2, 2)),
+            pltpu.VMEM((4 * NEAR, LOC * ZM // 2), BF16),
+            pltpu.VMEM((LOC, 2, N, 2 * ZM), BF16),
+            pltpu.SemaphoreType.DMA((2, 4)),
         ],
         compiler_params=params(24),
         name="last",

time: 114 us -> 113 us (level)
  no operation moved by 1% of the time
where the time goes in v3:
time: 113 us
  blocking collectives  42.5 us (38%)
  waiting for transfers between devices  32.8 us (29%)
  Pallas kernels  23.5 us (21%)
  starting transfers between devices  13.1 us (12%)
    all_to_all x2, blocking collectives, exchange(): lax.all_to_all(value, 'grid', split_axis=0, concat_axis=0, tiled=True)  42.5 us
    all_to_all x1, waiting for transfers between devices, exchange(): lax.all_to_all(value, 'grid', split_axis=0, concat_axis=0, tiled=True)  28.9 us
    pallas_call x1, Pallas kernels, shards(): pl.pallas_call(plane_kernel, out_shape=jax.ShapeDtypeStruct(flat, F32), g...  13.8 us
    all_to_all x1, starting transfers between devices, exchange(): lax.all_to_all(value, 'grid', split_axis=0, concat_axis=0, tiled=True)  8.29 us
    pallas_call x1, Pallas kernels, shards(): pl.pallas_call(first_kernel, out_shape=jax.ShapeDtypeStruct(message, F32)...  5.71 us
    ppermute x2, starting transfers between devices, shards(): lax.ppermute(hist, 'traj', [(t, t ^ bit) for t in range(TRAJ)])  4.84 us
    pallas_call x1, Pallas kernels, shards(): pl.pallas_call(last_kernel, out_shape=(jax.ShapeDtypeStruct(psi_modes.sha...  4.02 us
    ppermute x2, waiting for transfers between devices, shards(): lax.ppermute(hist, 'traj', [(t, t ^ bit) for t in range(TRAJ)])  3.87 us
  transfers between devices with their start and end apart: 3, of which 3 were waited for; matrix products, arithmetic and copies ran while one was open for 0% of the time, Pallas kernels for 0%

profile of v3, /device:TPU:0, one launch (start us, length us, event | category | flops | bytes accessed | tf_op | source)
XLA Modules:
  0.0 113.2 jit_solution(9073930454695281472)
XLA Ops:
  0.6 5.7 %first.1 = f32[32,2,8,8,128]{4,3,2,1,0:T(8,128)} custom-call(f32[1,2,256,8,256]{4,3,2,1,0:T(8,128)} %psi_hbm.1, s32[256,8,256]{2,1,0:T(8,128)} %mask_ref.1, bf16[8,512,256]{2,1,0:T(8,128)(2,1)} %constant.10.clone.table_hbm.tables_hbm.table_ref), custom_call_target="tpu_custom_call" | custom-call | tf_op jit(solution)/shard_map/first/pallas_call | solution.py:371
  6.3 8.3 %all-to-all-start = ((f32[32,2,8,8,128]{4,3,2,1,0:T(8,128)}), f32[32,2,8,8,128]{4,3,2,1,0:T(8,128)S(1)}, u32[]{:S(2)}, u32[]{:S(2)}) async-start(f32[32,2,8,8,128]{4,3,2,1,0:T(8,128)} %first.1), calls=%async_computation | async-start | bytes 4194304 | tf_op jit(solution)/shard_map/all_to_all | solution.py:360
  14.6 28.9 %all-to-all-done = f32[32,2,8,8,128]{4,3,2,1,0:T(8,128)S(1)} async-done(((f32[32,2,8,8,128]{4,3,2,1,0:T(8,128)}), f32[32,2,8,8,128]{4,3,2,1,0:T(8,128)S(1)}, u32[]{:S(2)}, u32[]{:S(2)}) %all-to-all-start) | async-done | bytes 2097184 | tf_op jit(solution)/shard_map/all_to_all | solution.py:360
  43.6 13.8 %planes.1 = f32[32,2,64,128]{3,2,1,0:T(8,128)S(1)} custom-call(s32[1]{0:T(128)} %bitcast.rank_ref, f32[32,2,64,128]{3,2,1,0:T(8,128)S(1)} %bitcast.8, f32[1,2,8,256,256]{4,3,2,1,0:T(8,128)} %noise_hbm.1, bf16[8,512,256]{2,1,0:T(8,128)(2,1)} %constant.10.clone.table_hbm.tables_hbm.table_ref), custom_call_target="tpu_custom_call" | custom-call | tf_op jit(solution)/shard_map/planes/pallas_call | solution.py:391
  57.4 0.0 copy-start
  57.4 0.0 copy-start.1
  57.4 31.3 %all_to_all.15 = f32[32,2,64,128]{3,2,1,0:T(8,128)S(1)} all-to-all(f32[32,2,64,128]{3,2,1,0:T(8,128)S(1)} %planes.1), channel_id=1, replica_groups=mesh['traj'=4,'grid'=32] {'grid'}, dimensions={0} | all-to-all | bytes 4194304 | tf_op jit(solution)/shard_map/all_to_all | solution.py:360
  88.7 0.0 copy-done
  88.7 0.0 copy-done.1
  88.7 4.0 %last.1 = (f32[1,2,256,8,256]{4,3,2,1,0:T(8,128)}, f32[32,1,128]{2,1,0:T(1,128)S(1)}) custom-call(s32[1]{0:T(128)} %bitcast.rank_ref, f32[32,2,8,8,128]{4,3,2,1,0:T(8,128)S(1)} %bitcast.7, s32[256,8,256]{2,1,0:T(8,128)S(1)} %copy-done.1, bf16[8,512,256]{2,1,0:T(8,128)(2,1)S(1)} %copy-done), custom_call_target="tpu_custom_call" | custom-call | tf_op jit(solution)/shard_map/last/pallas_call | solution.py:412
  92.7 11.2 %all_to_all.16 = f32[32,1,128]{2,1,0:T(1,128)S(1)} all-to-all(f32[32,1,128]{2,1,0:T(1,128)S(1)} %get-tuple-element.5), channel_id=1, replica_groups=mesh['traj'=4,'grid'=32] {'grid'}, dimensions={0} | all-to-all | bytes 32768 | tf_op jit(solution)/shard_map/all_to_all | solution.py:360
  104.0 0.1 reduce_sum.11
  104.0 1.6 %collective-permute-start = (f32[1,128]{1,0:T(1,128)S(1)}, f32[1,128]{1,0:T(1,128)S(1)}, u32[]{:S(2)}, u32[]{:S(2)}) collective-permute-start(f32[1,128]{1,0:T(1,128)S(1)} %bitcast.9), channel_id=1, source_target_pairs={{0,32},{32,0},{64,96},{96,64},{1,33},{33,1},{65,97},{97,65},{2,34}... | collective-permute-start | bytes 1544 | tf_op jit(solution)/shard_map/ppermute | solution.py:433
  105.7 2.0 %collective-permute-done = f32[1,128]{1,0:T(1,128)S(1)} collective-permute-done((f32[1,128]{1,0:T(1,128)S(1)}, f32[1,128]{1,0:T(1,128)S(1)}, u32[]{:S(2)}, u32[]{:S(2)}) %collective-permute-start) | collective-permute-done | bytes 544 | tf_op jit(solution)/shard_map/ppermute | solution.py:433
  107.7 3.2 %collective-permute-start.1 = (f32[1,128]{1,0:T(1,128)S(1)}, f32[1,128]{1,0:T(1,128)S(1)}, u32[]{:S(2)}, u32[]{:S(2)}) collective-permute-start(f32[1,128]{1,0:T(1,128)S(1)} %bitcast_add_fusion), channel_id=1, source_target_pairs={{0,64},{32,96},{64,0},{96,32},{1,65},{33,97},{65,1},{97,33},{2,66}... | collective-permute-start | bytes 1544 | tf_op jit(solution)/shard_map/ppermute | solution.py:433
  110.9 1.9 %collective-permute-done.1 = f32[1,128]{1,0:T(1,128)S(1)} collective-permute-done((f32[1,128]{1,0:T(1,128)S(1)}, f32[1,128]{1,0:T(1,128)S(1)}, u32[]{:S(2)}, u32[]{:S(2)}) %collective-permute-start.1) | collective-permute-done | bytes 544 | tf_op jit(solution)/shard_map/ppermute | solution.py:433
  112.7 0.5 multiply_bitcast_fusion
  (1 shorter events, 0.0 us)
Async XLA Ops:
  6.3 37.2 %all-to-all-start = ((f32[32,2,8,8,128]{4,3,2,1,0:T(8,128)}), f32[32,2,8,8,128]{4,3,2,1,0:T(8,128)S(1)}, u32[]{:S(2)}, u32[]{:S(2)}) async-start(f32[32,2,8,8,128]{4,3,2,1,0:T(8,128)} %first.1), calls=%async_computation | async-start | bytes 4194304 | tf_op jit(solution)/shard_map/all_to_all | solution.py:360
  57.4 31.3 %copy-start = (bf16[8,512,256]{2,1,0:T(8,128)(2,1)S(1)}, bf16[8,512,256]{2,1,0:T(8,128)(2,1)}, u32[]{:S(2)}) copy-start(bf16[8,512,256]{2,1,0:T(8,128)(2,1)} %constant.10.clone.table_hbm.tables_hbm.table_ref) | copy-start | bytes 6291460
  57.4 31.3 %copy-start.1 = (s32[256,8,256]{2,1,0:T(8,128)S(1)}, s32[256,8,256]{2,1,0:T(8,128)}, u32[]{:S(2)}) copy-start(s32[256,8,256]{2,1,0:T(8,128)} %mask_ref.1) | copy-start | bytes 6291460
  104.0 3.6 %collective-permute-start = (f32[1,128]{1,0:T(1,128)S(1)}, f32[1,128]{1,0:T(1,128)S(1)}, u32[]{:S(2)}, u32[]{:S(2)}) collective-permute-start(f32[1,128]{1,0:T(1,128)S(1)} %bitcast.9), channel_id=1, source_target_pairs={{0,32},{32,0},{64,96},{96,64},{1,33},{33,1},{65,97},{97,65},{2,34}... | collective-permute-start | bytes 1544 | tf_op jit(solution)/shard_map/ppermute | solution.py:433
  107.7 5.1 %collective-permute-start.1 = (f32[1,128]{1,0:T(1,128)S(1)}, f32[1,128]{1,0:T(1,128)S(1)}, u32[]{:S(2)}, u32[]{:S(2)}) collective-permute-start(f32[1,128]{1,0:T(1,128)S(1)} %bitcast_add_fusion), channel_id=1, source_target_pairs={{0,64},{32,96},{64,0},{96,32},{1,65},{33,97},{65,1},{97,33},{2,66}... | collective-permute-start | bytes 1544 | tf_op jit(solution)/shard_map/ppermute | solution.py:433

commit v4 on v3

--- a/solution.py
+++ b/solution.py
@@ -115,8 +115,6 @@
         for copy in pair:
             copy.start()
     table_copy.start()
-    for copy in copies[2]:
-        copy.start()
     table = None
     sent = []
     for half in range(2):
@@ -127,6 +125,8 @@
                 copies[0][piece].wait()
                 keep[lines] = select_tiles(mask[part]).astype(F32).reshape(count * LOC, ZM)
             copies[1 + half][piece].wait()
+            if half == 0:
+                copies[2][piece].start()
             field[half, lines] = select_tiles(psi[half, part]).reshape(count * LOC, ZM) * keep[lines]
         if half == 0:
             table_copy.wait()
@@ -208,18 +208,18 @@
 
     @pl.when(step == 0)
     def _():
-        for copy in table_copies[:2]:
-            copy.start()
-        noise_copy(0).start()
-        table_copies[2].start()
-        for later in range(1, groups):
-            noise_copy(later).start()
+        table_copies[0].start()
+        table_copies[1].start()
         shape = (N, N)
         pos_y = (lax.broadcasted_iota(jnp.int32, shape, 0).astype(F32) + 0.5) / N - 0.5
         pos_z = (lax.broadcasted_iota(jnp.int32, shape, 1).astype(F32) + 0.5) / N - 0.5
         base[...] = TURN * (trap_strength * (pos_y * pos_y + pos_z * pos_z) - chem_potential)
-        for copy in table_copies[:2]:
-            copy.wait()
+        table_copies[0].wait()
+        noise_copy(0).start()
+        table_copies[2].start()
+        table_copies[1].wait()
+        for later in range(1, groups):
+            noise_copy(later).start()
 
     field = to_field(step)
     noise_copy(step).wait()
@@ -429,8 +429,8 @@
         name="last",
     )(rank, rows_in, mask, tables)
     hist = jnp.sum(exchange(hist), axis=0)
-    for bit in (1, 2):
-        hist = hist + lax.ppermute(hist, "traj", [(t, t ^ bit) for t in range(TRAJ)])
+    other = [lax.ppermute(hist, "traj", [(t, (t + k) % TRAJ) for t in range(TRAJ)]) for k in (1, 2, 3)]
+    hist = (hist + other[1]) + (other[0] + other[2])
     return psi_next, hist.reshape(SHELLS) * (SHELLS / (TRAJ * N * N * N))
 
 

time: 113 us -> 113 us (level)
    ppermute x2 -> x3, waiting for transfers between devices: 3.87 us -> 3.09 us  [shards(): lax.ppermute(hist, 'traj', [(t, (t + k) % TRAJ) for t in range(TRAJ)])]
    ppermute x2 -> x3, starting transfers between devices: 4.84 us -> 5.28 us  [shards(): lax.ppermute(hist, 'traj', [(t, (t + k) % TRAJ) for t in range(TRAJ)])]
  transfers between devices with their start and end apart: 3 -> 4, of which waited for: 3 -> 2; matrix products, arithmetic and copies ran while one was open for 0% -> 0% of each run, Pallas kernels for 0% -> 0%
where the time goes in v4:
time: 113 us
  blocking collectives  42.5 us (38%)
  waiting for transfers between devices  32 us (28%)
  Pallas kernels  23.5 us (21%)
  starting transfers between devices  13.6 us (12%)
    all_to_all x2, blocking collectives, exchange(): lax.all_to_all(value, 'grid', split_axis=0, concat_axis=0, tiled=True)  42.5 us
    all_to_all x1, waiting for transfers between devices, exchange(): lax.all_to_all(value, 'grid', split_axis=0, concat_axis=0, tiled=True)  28.9 us
    pallas_call x1, Pallas kernels, shards(): pl.pallas_call(plane_kernel, out_shape=jax.ShapeDtypeStruct(flat, F32), g...  13.8 us
    all_to_all x1, starting transfers between devices, exchange(): lax.all_to_all(value, 'grid', split_axis=0, concat_axis=0, tiled=True)  8.29 us
    pallas_call x1, Pallas kernels, shards(): pl.pallas_call(first_kernel, out_shape=jax.ShapeDtypeStruct(message, F32)...  5.71 us
    ppermute x3, starting transfers between devices, shards(): lax.ppermute(hist, 'traj', [(t, (t + k) % TRAJ) for t in range(TRAJ)])  5.28 us
    pallas_call x1, Pallas kernels, shards(): pl.pallas_call(last_kernel, out_shape=(jax.ShapeDtypeStruct(psi_modes.sha...  4.02 us
    ppermute x3, waiting for transfers between devices, shards(): lax.ppermute(hist, 'traj', [(t, (t + k) % TRAJ) for t in range(TRAJ)])  3.09 us
  transfers between devices with their start and end apart: 4, of which 2 were waited for; matrix products, arithmetic and copies ran while one was open for 0% of the time, Pallas kernels for 0%

profile of v4, /device:TPU:0, one launch (start us, length us, event | category | flops | bytes accessed | tf_op | source)
XLA Modules:
  0.0 112.9 jit_solution(7736483215410142833)
XLA Ops:
  0.6 5.7 %first.1 = f32[32,2,8,8,128]{4,3,2,1,0:T(8,128)} custom-call(f32[1,2,256,8,256]{4,3,2,1,0:T(8,128)} %psi_hbm.1, s32[256,8,256]{2,1,0:T(8,128)} %mask_ref.1, bf16[8,512,256]{2,1,0:T(8,128)(2,1)} %constant.10.clone.table_hbm.tables_hbm.table_ref), custom_call_target="tpu_custom_call" | custom-call | tf_op jit(solution)/shard_map/first/pallas_call | solution.py:371
  6.3 8.3 %all-to-all-start = ((f32[32,2,8,8,128]{4,3,2,1,0:T(8,128)}), f32[32,2,8,8,128]{4,3,2,1,0:T(8,128)S(1)}, u32[]{:S(2)}, u32[]{:S(2)}) async-start(f32[32,2,8,8,128]{4,3,2,1,0:T(8,128)} %first.1), calls=%async_computation | async-start | bytes 4194304 | tf_op jit(solution)/shard_map/all_to_all | solution.py:360
  14.6 28.9 %all-to-all-done = f32[32,2,8,8,128]{4,3,2,1,0:T(8,128)S(1)} async-done(((f32[32,2,8,8,128]{4,3,2,1,0:T(8,128)}), f32[32,2,8,8,128]{4,3,2,1,0:T(8,128)S(1)}, u32[]{:S(2)}, u32[]{:S(2)}) %all-to-all-start) | async-done | bytes 2097184 | tf_op jit(solution)/shard_map/all_to_all | solution.py:360
  43.6 13.8 %planes.1 = f32[32,2,64,128]{3,2,1,0:T(8,128)S(1)} custom-call(s32[1]{0:T(128)} %bitcast.rank_ref, f32[32,2,64,128]{3,2,1,0:T(8,128)S(1)} %bitcast.8, f32[1,2,8,256,256]{4,3,2,1,0:T(8,128)} %noise_hbm.1, bf16[8,512,256]{2,1,0:T(8,128)(2,1)} %constant.10.clone.table_hbm.tables_hbm.table_ref), custom_call_target="tpu_custom_call" | custom-call | tf_op jit(solution)/shard_map/planes/pallas_call | solution.py:391
  57.4 0.0 copy-start
  57.4 0.0 copy-start.1
  57.4 31.3 %all_to_all.15 = f32[32,2,64,128]{3,2,1,0:T(8,128)S(1)} all-to-all(f32[32,2,64,128]{3,2,1,0:T(8,128)S(1)} %planes.1), channel_id=1, replica_groups=mesh['traj'=4,'grid'=32] {'grid'}, dimensions={0} | all-to-all | bytes 4194304 | tf_op jit(solution)/shard_map/all_to_all | solution.py:360
  88.7 0.0 copy-done
  88.7 0.0 copy-done.1
  88.7 4.0 %last.1 = (f32[1,2,256,8,256]{4,3,2,1,0:T(8,128)}, f32[32,1,128]{2,1,0:T(1,128)S(1)}) custom-call(s32[1]{0:T(128)} %bitcast.rank_ref, f32[32,2,8,8,128]{4,3,2,1,0:T(8,128)S(1)} %bitcast.7, s32[256,8,256]{2,1,0:T(8,128)S(1)} %copy-done.1, bf16[8,512,256]{2,1,0:T(8,128)(2,1)S(1)} %copy-done), custom_call_target="tpu_custom_call" | custom-call | tf_op jit(solution)/shard_map/last/pallas_call | solution.py:412
  92.7 11.2 %all_to_all.16 = f32[32,1,128]{2,1,0:T(1,128)S(1)} all-to-all(f32[32,1,128]{2,1,0:T(1,128)S(1)} %get-tuple-element.5), channel_id=1, replica_groups=mesh['traj'=4,'grid'=32] {'grid'}, dimensions={0} | all-to-all | bytes 32768 | tf_op jit(solution)/shard_map/all_to_all | solution.py:360
  104.0 0.1 reduce_sum.11
  104.0 1.6 %collective-permute-start.1 = (f32[1,128]{1,0:T(1,128)S(1)}, f32[1,128]{1,0:T(1,128)S(1)}, u32[]{:S(2)}, u32[]{:S(2)}) collective-permute-start(f32[1,128]{1,0:T(1,128)S(1)} %bitcast.9), channel_id=1, source_target_pairs={{0,32},{32,64},{64,96},{96,0},{1,33},{33,65},{65,97},{97,1},{2,34}... | collective-permute-start | bytes 1544 | tf_op jit(solution)/shard_map/ppermute | solution.py:432
  105.7 1.7 %collective-permute-start.2 = (f32[1,128]{1,0:T(1,128)S(1)}, f32[1,128]{1,0:T(1,128)S(1)}, u32[]{:S(2)}, u32[]{:S(2)}) collective-permute-start(f32[1,128]{1,0:T(1,128)S(1)} %bitcast.10), channel_id=1, source_target_pairs={{0,96},{32,0},{64,32},{96,64},{1,97},{33,1},{65,33},{97,65},{2,98}... | collective-permute-start | bytes 1544 | tf_op jit(solution)/shard_map/ppermute | solution.py:432
  107.3 2.0 %collective-permute-start = (f32[1,128]{1,0:T(1,128)S(1)}, f32[1,128]{1,0:T(1,128)S(1)}, u32[]{:S(2)}, u32[]{:S(2)}) collective-permute-start(f32[1,128]{1,0:T(1,128)S(1)} %bitcast.11), channel_id=1, source_target_pairs={{0,64},{32,96},{64,0},{96,32},{1,65},{33,97},{65,1},{97,33},{2,66}... | collective-permute-start | bytes 1544 | tf_op jit(solution)/shard_map/ppermute | solution.py:432
  109.3 0.0 collective-permute-done.1
  109.3 0.0 collective-permute-done.2
  109.3 3.1 %collective-permute-done = f32[1,128]{1,0:T(1,128)S(1)} collective-permute-done((f32[1,128]{1,0:T(1,128)S(1)}, f32[1,128]{1,0:T(1,128)S(1)}, u32[]{:S(2)}, u32[]{:S(2)}) %collective-permute-start) | collective-permute-done | bytes 544 | tf_op jit(solution)/shard_map/ppermute | solution.py:432
  112.4 0.5 multiply_bitcast_fusion
Async XLA Ops:
  6.3 37.2 %all-to-all-start = ((f32[32,2,8,8,128]{4,3,2,1,0:T(8,128)}), f32[32,2,8,8,128]{4,3,2,1,0:T(8,128)S(1)}, u32[]{:S(2)}, u32[]{:S(2)}) async-start(f32[32,2,8,8,128]{4,3,2,1,0:T(8,128)} %first.1), calls=%async_computation | async-start | bytes 4194304 | tf_op jit(solution)/shard_map/all_to_all | solution.py:360
  57.4 31.3 %copy-start = (bf16[8,512,256]{2,1,0:T(8,128)(2,1)S(1)}, bf16[8,512,256]{2,1,0:T(8,128)(2,1)}, u32[]{:S(2)}) copy-start(bf16[8,512,256]{2,1,0:T(8,128)(2,1)} %constant.10.clone.table_hbm.tables_hbm.table_ref) | copy-start | bytes 6291460
  57.4 31.3 %copy-start.1 = (s32[256,8,256]{2,1,0:T(8,128)S(1)}, s32[256,8,256]{2,1,0:T(8,128)}, u32[]{:S(2)}) copy-start(s32[256,8,256]{2,1,0:T(8,128)} %mask_ref.1) | copy-start | bytes 6291460
  104.0 5.3 %collective-permute-start.1 = (f32[1,128]{1,0:T(1,128)S(1)}, f32[1,128]{1,0:T(1,128)S(1)}, u32[]{:S(2)}, u32[]{:S(2)}) collective-permute-start(f32[1,128]{1,0:T(1,128)S(1)} %bitcast.9), channel_id=1, source_target_pairs={{0,32},{32,64},{64,96},{96,0},{1,33},{33,65},{65,97},{97,1},{2,34}... | collective-permute-start | bytes 1544 | tf_op jit(solution)/shard_map/ppermute | solution.py:432
  105.7 3.7 %collective-permute-start.2 = (f32[1,128]{1,0:T(1,128)S(1)}, f32[1,128]{1,0:T(1,128)S(1)}, u32[]{:S(2)}, u32[]{:S(2)}) collective-permute-start(f32[1,128]{1,0:T(1,128)S(1)} %bitcast.10), channel_id=1, source_target_pairs={{0,96},{32,0},{64,32},{96,64},{1,97},{33,1},{65,33},{97,65},{2,98}... | collective-permute-start | bytes 1544 | tf_op jit(solution)/shard_map/ppermute | solution.py:432
  107.3 5.1 %collective-permute-start = (f32[1,128]{1,0:T(1,128)S(1)}, f32[1,128]{1,0:T(1,128)S(1)}, u32[]{:S(2)}, u32[]{:S(2)}) collective-permute-start(f32[1,128]{1,0:T(1,128)S(1)} %bitcast.11), channel_id=1, source_target_pairs={{0,64},{32,96},{64,0},{96,32},{1,65},{33,97},{65,1},{97,33},{2,66}... | collective-permute-start | bytes 1544 | tf_op jit(solution)/shard_map/ppermute | solution.py:432

commit v5 on v4

--- a/solution.py
+++ b/solution.py
@@ -13,7 +13,7 @@
 ZM = N // 2
 TRAJ = 4
 PLANES_MIB = 48
-STEP_PLANES = 4
+STEP_PLANES = 8
 
 time_step = 1.0
 damping = 0.05

time: 113 us -> 113 us (level)
  no operation moved by 1% of the time
where the time goes in v5:
time: 113 us
  blocking collectives  42.6 us (38%)
  waiting for transfers between devices  31.8 us (28%)
  Pallas kernels  23.1 us (20%)
  starting transfers between devices  13.7 us (12%)
    all_to_all x2, blocking collectives, exchange(): lax.all_to_all(value, 'grid', split_axis=0, concat_axis=0, tiled=True)  42.6 us
    all_to_all x1, waiting for transfers between devices, exchange(): lax.all_to_all(value, 'grid', split_axis=0, concat_axis=0, tiled=True)  28.7 us
    pallas_call x1, Pallas kernels, shards(): pl.pallas_call(plane_kernel, out_shape=jax.ShapeDtypeStruct(flat, F32), g...  13.4 us
    all_to_all x1, starting transfers between devices, exchange(): lax.all_to_all(value, 'grid', split_axis=0, concat_axis=0, tiled=True)  8.47 us
    pallas_call x1, Pallas kernels, shards(): pl.pallas_call(first_kernel, out_shape=jax.ShapeDtypeStruct(message, F32)...  5.71 us
    ppermute x3, starting transfers between devices, shards(): lax.ppermute(hist, 'traj', [(t, (t + k) % TRAJ) for t in range(TRAJ)])  5.28 us
    pallas_call x1, Pallas kernels, shards(): pl.pallas_call(last_kernel, out_shape=(jax.ShapeDtypeStruct(psi_modes.sha...  4.02 us
    ppermute x3, waiting for transfers between devices, shards(): lax.ppermute(hist, 'traj', [(t, (t + k) % TRAJ) for t in range(TRAJ)])  3.09 us
  transfers between devices with their start and end apart: 4, of which 2 were waited for; matrix products, arithmetic and copies ran while one was open for 0% of the time, Pallas kernels for 0%

profile of v5, /device:TPU:0, one launch (start us, length us, event | category | flops | bytes accessed | tf_op | source)
XLA Modules:
  0.0 112.5 jit_solution(11946966898454120239)
XLA Ops:
  0.6 5.7 %first.1 = f32[32,2,8,8,128]{4,3,2,1,0:T(8,128)} custom-call(f32[1,2,256,8,256]{4,3,2,1,0:T(8,128)} %psi_hbm.1, s32[256,8,256]{2,1,0:T(8,128)} %mask_ref.1, bf16[8,512,256]{2,1,0:T(8,128)(2,1)} %constant.10.clone.table_hbm.tables_hbm.table_ref), custom_call_target="tpu_custom_call" | custom-call | tf_op jit(solution)/shard_map/first/pallas_call | solution.py:371
  6.3 8.5 %all-to-all-start = ((f32[32,2,8,8,128]{4,3,2,1,0:T(8,128)}), f32[32,2,8,8,128]{4,3,2,1,0:T(8,128)S(1)}, u32[]{:S(2)}, u32[]{:S(2)}) async-start(f32[32,2,8,8,128]{4,3,2,1,0:T(8,128)} %first.1), calls=%async_computation | async-start | bytes 4194304 | tf_op jit(solution)/shard_map/all_to_all | solution.py:360
  14.8 28.7 %all-to-all-done = f32[32,2,8,8,128]{4,3,2,1,0:T(8,128)S(1)} async-done(((f32[32,2,8,8,128]{4,3,2,1,0:T(8,128)}), f32[32,2,8,8,128]{4,3,2,1,0:T(8,128)S(1)}, u32[]{:S(2)}, u32[]{:S(2)}) %all-to-all-start) | async-done | bytes 2097184 | tf_op jit(solution)/shard_map/all_to_all | solution.py:360
  43.6 13.4 %planes.1 = f32[32,2,64,128]{3,2,1,0:T(8,128)S(1)} custom-call(s32[1]{0:T(128)} %bitcast.rank_ref, f32[32,2,64,128]{3,2,1,0:T(8,128)S(1)} %bitcast.8, f32[1,2,8,256,256]{4,3,2,1,0:T(8,128)} %noise_hbm.1, bf16[8,512,256]{2,1,0:T(8,128)(2,1)} %constant.10.clone.table_hbm.tables_hbm.table_ref), custom_call_target="tpu_custom_call" | custom-call | tf_op jit(solution)/shard_map/planes/pallas_call | solution.py:391
  57.0 0.0 copy-start
  57.0 0.0 copy-start.1
  57.0 31.3 %all_to_all.15 = f32[32,2,64,128]{3,2,1,0:T(8,128)S(1)} all-to-all(f32[32,2,64,128]{3,2,1,0:T(8,128)S(1)} %planes.1), channel_id=1, replica_groups=mesh['traj'=4,'grid'=32] {'grid'}, dimensions={0} | all-to-all | bytes 4194304 | tf_op jit(solution)/shard_map/all_to_all | solution.py:360
  88.3 0.0 copy-done
  88.3 0.0 copy-done.1
  88.3 4.0 %last.1 = (f32[1,2,256,8,256]{4,3,2,1,0:T(8,128)}, f32[32,1,128]{2,1,0:T(1,128)S(1)}) custom-call(s32[1]{0:T(128)} %bitcast.rank_ref, f32[32,2,8,8,128]{4,3,2,1,0:T(8,128)S(1)} %bitcast.7, s32[256,8,256]{2,1,0:T(8,128)S(1)} %copy-done.1, bf16[8,512,256]{2,1,0:T(8,128)(2,1)S(1)} %copy-done), custom_call_target="tpu_custom_call" | custom-call | tf_op jit(solution)/shard_map/last/pallas_call | solution.py:412
  92.3 11.2 %all_to_all.16 = f32[32,1,128]{2,1,0:T(1,128)S(1)} all-to-all(f32[32,1,128]{2,1,0:T(1,128)S(1)} %get-tuple-element.5), channel_id=1, replica_groups=mesh['traj'=4,'grid'=32] {'grid'}, dimensions={0} | all-to-all | bytes 32768 | tf_op jit(solution)/shard_map/all_to_all | solution.py:360
  103.6 0.1 reduce_sum.11
  103.6 1.6 %collective-permute-start.1 = (f32[1,128]{1,0:T(1,128)S(1)}, f32[1,128]{1,0:T(1,128)S(1)}, u32[]{:S(2)}, u32[]{:S(2)}) collective-permute-start(f32[1,128]{1,0:T(1,128)S(1)} %bitcast.9), channel_id=1, source_target_pairs={{0,32},{32,64},{64,96},{96,0},{1,33},{33,65},{65,97},{97,1},{2,34}... | collective-permute-start | bytes 1544 | tf_op jit(solution)/shard_map/ppermute | solution.py:432
  105.3 1.7 %collective-permute-start.2 = (f32[1,128]{1,0:T(1,128)S(1)}, f32[1,128]{1,0:T(1,128)S(1)}, u32[]{:S(2)}, u32[]{:S(2)}) collective-permute-start(f32[1,128]{1,0:T(1,128)S(1)} %bitcast.10), channel_id=1, source_target_pairs={{0,96},{32,0},{64,32},{96,64},{1,97},{33,1},{65,33},{97,65},{2,98}... | collective-permute-start | bytes 1544 | tf_op jit(solution)/shard_map/ppermute | solution.py:432
  106.9 2.0 %collective-permute-start = (f32[1,128]{1,0:T(1,128)S(1)}, f32[1,128]{1,0:T(1,128)S(1)}, u32[]{:S(2)}, u32[]{:S(2)}) collective-permute-start(f32[1,128]{1,0:T(1,128)S(1)} %bitcast.11), channel_id=1, source_target_pairs={{0,64},{32,96},{64,0},{96,32},{1,65},{33,97},{65,1},{97,33},{2,66}... | collective-permute-start | bytes 1544 | tf_op jit(solution)/shard_map/ppermute | solution.py:432
  108.9 0.0 collective-permute-done.1
  108.9 0.0 collective-permute-done.2
  108.9 3.1 %collective-permute-done = f32[1,128]{1,0:T(1,128)S(1)} collective-permute-done((f32[1,128]{1,0:T(1,128)S(1)}, f32[1,128]{1,0:T(1,128)S(1)}, u32[]{:S(2)}, u32[]{:S(2)}) %collective-permute-start) | collective-permute-done | bytes 544 | tf_op jit(solution)/shard_map/ppermute | solution.py:432
  112.0 0.5 multiply_bitcast_fusion
Async XLA Ops:
  6.3 37.2 %all-to-all-start = ((f32[32,2,8,8,128]{4,3,2,1,0:T(8,128)}), f32[32,2,8,8,128]{4,3,2,1,0:T(8,128)S(1)}, u32[]{:S(2)}, u32[]{:S(2)}) async-start(f32[32,2,8,8,128]{4,3,2,1,0:T(8,128)} %first.1), calls=%async_computation | async-start | bytes 4194304 | tf_op jit(solution)/shard_map/all_to_all | solution.py:360
  57.0 31.3 %copy-start = (bf16[8,512,256]{2,1,0:T(8,128)(2,1)S(1)}, bf16[8,512,256]{2,1,0:T(8,128)(2,1)}, u32[]{:S(2)}) copy-start(bf16[8,512,256]{2,1,0:T(8,128)(2,1)} %constant.10.clone.table_hbm.tables_hbm.table_ref) | copy-start | bytes 6291460
  57.0 31.3 %copy-start.1 = (s32[256,8,256]{2,1,0:T(8,128)S(1)}, s32[256,8,256]{2,1,0:T(8,128)}, u32[]{:S(2)}) copy-start(s32[256,8,256]{2,1,0:T(8,128)} %mask_ref.1) | copy-start | bytes 6291460
  103.6 5.3 %collective-permute-start.1 = (f32[1,128]{1,0:T(1,128)S(1)}, f32[1,128]{1,0:T(1,128)S(1)}, u32[]{:S(2)}, u32[]{:S(2)}) collective-permute-start(f32[1,128]{1,0:T(1,128)S(1)} %bitcast.9), channel_id=1, source_target_pairs={{0,32},{32,64},{64,96},{96,0},{1,33},{33,65},{65,97},{97,1},{2,34}... | collective-permute-start | bytes 1544 | tf_op jit(solution)/shard_map/ppermute | solution.py:432
  105.3 3.7 %collective-permute-start.2 = (f32[1,128]{1,0:T(1,128)S(1)}, f32[1,128]{1,0:T(1,128)S(1)}, u32[]{:S(2)}, u32[]{:S(2)}) collective-permute-start(f32[1,128]{1,0:T(1,128)S(1)} %bitcast.10), channel_id=1, source_target_pairs={{0,96},{32,0},{64,32},{96,64},{1,97},{33,1},{65,33},{97,65},{2,98}... | collective-permute-start | bytes 1544 | tf_op jit(solution)/shard_map/ppermute | solution.py:432
  106.9 5.1 %collective-permute-start = (f32[1,128]{1,0:T(1,128)S(1)}, f32[1,128]{1,0:T(1,128)S(1)}, u32[]{:S(2)}, u32[]{:S(2)}) collective-permute-start(f32[1,128]{1,0:T(1,128)S(1)} %bitcast.11), channel_id=1, source_target_pairs={{0,64},{32,96},{64,0},{96,32},{1,65},{33,97},{65,1},{97,33},{2,66}... | collective-permute-start | bytes 1544 | tf_op jit(solution)/shard_map/ppermute | solution.py:432

commit v6 on v5

--- a/solution.py
+++ b/solution.py
@@ -131,9 +131,9 @@
         if half == 0:
             table_copy.wait()
             table = (table_ref[0], table_ref[1])
-        for pair in range(LOC // 2):
+        for pair in range(LOC // 4):
             value = jnp.concatenate(
-                [field[half, pl.ds(2 * pair + k, N, stride=LOC), :] for k in range(2)], axis=1
+                [field[half, pl.ds(4 * pair + k, N, stride=LOC), :] for k in range(4)], axis=1
             )
             value = dot3(table, split(value))
             if half == 0:
@@ -141,11 +141,11 @@
             else:
                 real = partial[pair, :N] - value[N:]
                 imag = partial[pair, N:] + value[:N]
-                for k in range(2):
+                for k in range(4):
                     lanes = slice(k * ZM, (k + 1) * ZM)
-                    out[:, 0, 2 * pair + k] = real[:, lanes].reshape(GRID, LOC, ZM)
-                    out[:, 1, 2 * pair + k] = imag[:, lanes].reshape(GRID, LOC, ZM)
-                rows = pl.ds(2 * pair, 2)
+                    out[:, 0, 4 * pair + k] = real[:, lanes].reshape(GRID, LOC, ZM)
+                    out[:, 1, 4 * pair + k] = imag[:, lanes].reshape(GRID, LOC, ZM)
+                rows = pl.ds(4 * pair, 4)
                 sent.append(pltpu.make_async_copy(out.at[:, :, rows], out_hbm.at[:, :, rows], sems.at[4, pair]))
                 sent[-1].start()
     for copy in sent:
@@ -380,7 +380,7 @@
             pltpu.VMEM((2, 2 * N, N), BF16),
             pltpu.VMEM((N * LOC, ZM), F32),
             pltpu.VMEM((2, N * LOC, ZM), F32),
-            pltpu.VMEM((LOC // 2, 2 * N, 2 * ZM), F32),
+            pltpu.VMEM((LOC // 4, 2 * N, 4 * ZM), F32),
             pltpu.VMEM(message, F32),
             pltpu.SemaphoreType.DMA((5, 4)),
         ],

time: 113 us -> 113 us (level)
  no operation moved by 1% of the time
where the time goes in v6:
time: 113 us; the launch traced here: 112 us
  blocking collectives  42.6 us (38%)
  waiting for transfers between devices  31.8 us (28%)
  Pallas kernels  23 us (20%)
  starting transfers between devices  13.7 us (12%)
    all_to_all x2, blocking collectives, exchange(): lax.all_to_all(value, 'grid', split_axis=0, concat_axis=0, tiled=True)  42.6 us
    all_to_all x1, waiting for transfers between devices, exchange(): lax.all_to_all(value, 'grid', split_axis=0, concat_axis=0, tiled=True)  28.7 us
    pallas_call x1, Pallas kernels, shards(): pl.pallas_call(plane_kernel, out_shape=jax.ShapeDtypeStruct(flat, F32), g...  13.4 us
    all_to_all x1, starting transfers between devices, exchange(): lax.all_to_all(value, 'grid', split_axis=0, concat_axis=0, tiled=True)  8.47 us
    pallas_call x1, Pallas kernels, shards(): pl.pallas_call(first_kernel, out_shape=jax.ShapeDtypeStruct(message, F32)...  5.63 us
    ppermute x3, starting transfers between devices, shards(): lax.ppermute(hist, 'traj', [(t, (t + k) % TRAJ) for t in range(TRAJ)])  5.28 us
    pallas_call x1, Pallas kernels, shards(): pl.pallas_call(last_kernel, out_shape=(jax.ShapeDtypeStruct(psi_modes.sha...  4.02 us
    ppermute x3, waiting for transfers between devices, shards(): lax.ppermute(hist, 'traj', [(t, (t + k) % TRAJ) for t in range(TRAJ)])  3.09 us
  transfers between devices with their start and end apart: 4, of which 2 were waited for; matrix products, arithmetic and copies ran while one was open for 0% of the time, Pallas kernels for 0%

profile of v6, /device:TPU:0, one launch (start us, length us, event | category | flops | bytes accessed | tf_op | source)
XLA Modules:
  0.0 112.4 jit_solution(778130786629325342)
XLA Ops:
  0.6 5.6 %first.1 = f32[32,2,8,8,128]{4,3,2,1,0:T(8,128)} custom-call(f32[1,2,256,8,256]{4,3,2,1,0:T(8,128)} %psi_hbm.1, s32[256,8,256]{2,1,0:T(8,128)} %mask_ref.1, bf16[8,512,256]{2,1,0:T(8,128)(2,1)} %constant.10.clone.table_hbm.tables_hbm.table_ref), custom_call_target="tpu_custom_call" | custom-call | tf_op jit(solution)/shard_map/first/pallas_call | solution.py:371
  6.3 8.5 %all-to-all-start = ((f32[32,2,8,8,128]{4,3,2,1,0:T(8,128)}), f32[32,2,8,8,128]{4,3,2,1,0:T(8,128)S(1)}, u32[]{:S(2)}, u32[]{:S(2)}) async-start(f32[32,2,8,8,128]{4,3,2,1,0:T(8,128)} %first.1), calls=%async_computation | async-start | bytes 4194304 | tf_op jit(solution)/shard_map/all_to_all | solution.py:360
  14.7 28.7 %all-to-all-done = f32[32,2,8,8,128]{4,3,2,1,0:T(8,128)S(1)} async-done(((f32[32,2,8,8,128]{4,3,2,1,0:T(8,128)}), f32[32,2,8,8,128]{4,3,2,1,0:T(8,128)S(1)}, u32[]{:S(2)}, u32[]{:S(2)}) %all-to-all-start) | async-done | bytes 2097184 | tf_op jit(solution)/shard_map/all_to_all | solution.py:360
  43.5 13.4 %planes.1 = f32[32,2,64,128]{3,2,1,0:T(8,128)S(1)} custom-call(s32[1]{0:T(128)} %bitcast.rank_ref, f32[32,2,64,128]{3,2,1,0:T(8,128)S(1)} %bitcast.8, f32[1,2,8,256,256]{4,3,2,1,0:T(8,128)} %noise_hbm.1, bf16[8,512,256]{2,1,0:T(8,128)(2,1)} %constant.10.clone.table_hbm.tables_hbm.table_ref), custom_call_target="tpu_custom_call" | custom-call | tf_op jit(solution)/shard_map/planes/pallas_call | solution.py:391
  56.9 0.0 copy-start
  56.9 0.0 copy-start.1
  56.9 31.3 %all_to_all.15 = f32[32,2,64,128]{3,2,1,0:T(8,128)S(1)} all-to-all(f32[32,2,64,128]{3,2,1,0:T(8,128)S(1)} %planes.1), channel_id=1, replica_groups=mesh['traj'=4,'grid'=32] {'grid'}, dimensions={0} | all-to-all | bytes 4194304 | tf_op jit(solution)/shard_map/all_to_all | solution.py:360
  88.2 0.0 copy-done
  88.2 0.0 copy-done.1
  88.2 4.0 %last.1 = (f32[1,2,256,8,256]{4,3,2,1,0:T(8,128)}, f32[32,1,128]{2,1,0:T(1,128)S(1)}) custom-call(s32[1]{0:T(128)} %bitcast.rank_ref, f32[32,2,8,8,128]{4,3,2,1,0:T(8,128)S(1)} %bitcast.7, s32[256,8,256]{2,1,0:T(8,128)S(1)} %copy-done.1, bf16[8,512,256]{2,1,0:T(8,128)(2,1)S(1)} %copy-done), custom_call_target="tpu_custom_call" | custom-call | tf_op jit(solution)/shard_map/last/pallas_call | solution.py:412
  92.3 11.2 %all_to_all.16 = f32[32,1,128]{2,1,0:T(1,128)S(1)} all-to-all(f32[32,1,128]{2,1,0:T(1,128)S(1)} %get-tuple-element.5), channel_id=1, replica_groups=mesh['traj'=4,'grid'=32] {'grid'}, dimensions={0} | all-to-all | bytes 32768 | tf_op jit(solution)/shard_map/all_to_all | solution.py:360
  103.5 0.1 reduce_sum.11
  103.6 1.6 %collective-permute-start.1 = (f32[1,128]{1,0:T(1,128)S(1)}, f32[1,128]{1,0:T(1,128)S(1)}, u32[]{:S(2)}, u32[]{:S(2)}) collective-permute-start(f32[1,128]{1,0:T(1,128)S(1)} %bitcast.9), channel_id=1, source_target_pairs={{0,32},{32,64},{64,96},{96,0},{1,33},{33,65},{65,97},{97,1},{2,34}... | collective-permute-start | bytes 1544 | tf_op jit(solution)/shard_map/ppermute | solution.py:432
  105.2 1.7 %collective-permute-start.2 = (f32[1,128]{1,0:T(1,128)S(1)}, f32[1,128]{1,0:T(1,128)S(1)}, u32[]{:S(2)}, u32[]{:S(2)}) collective-permute-start(f32[1,128]{1,0:T(1,128)S(1)} %bitcast.10), channel_id=1, source_target_pairs={{0,96},{32,0},{64,32},{96,64},{1,97},{33,1},{65,33},{97,65},{2,98}... | collective-permute-start | bytes 1544 | tf_op jit(solution)/shard_map/ppermute | solution.py:432
  106.8 2.0 %collective-permute-start = (f32[1,128]{1,0:T(1,128)S(1)}, f32[1,128]{1,0:T(1,128)S(1)}, u32[]{:S(2)}, u32[]{:S(2)}) collective-permute-start(f32[1,128]{1,0:T(1,128)S(1)} %bitcast.11), channel_id=1, source_target_pairs={{0,64},{32,96},{64,0},{96,32},{1,65},{33,97},{65,1},{97,33},{2,66}... | collective-permute-start | bytes 1544 | tf_op jit(solution)/shard_map/ppermute | solution.py:432
  108.8 0.0 collective-permute-done.1
  108.8 0.0 collective-permute-done.2
  108.8 3.1 %collective-permute-done = f32[1,128]{1,0:T(1,128)S(1)} collective-permute-done((f32[1,128]{1,0:T(1,128)S(1)}, f32[1,128]{1,0:T(1,128)S(1)}, u32[]{:S(2)}, u32[]{:S(2)}) %collective-permute-start) | collective-permute-done | bytes 544 | tf_op jit(solution)/shard_map/ppermute | solution.py:432
  111.9 0.5 multiply_bitcast_fusion
Async XLA Ops:
  6.3 37.2 %all-to-all-start = ((f32[32,2,8,8,128]{4,3,2,1,0:T(8,128)}), f32[32,2,8,8,128]{4,3,2,1,0:T(8,128)S(1)}, u32[]{:S(2)}, u32[]{:S(2)}) async-start(f32[32,2,8,8,128]{4,3,2,1,0:T(8,128)} %first.1), calls=%async_computation | async-start | bytes 4194304 | tf_op jit(solution)/shard_map/all_to_all | solution.py:360
  56.9 31.3 %copy-start = (bf16[8,512,256]{2,1,0:T(8,128)(2,1)S(1)}, bf16[8,512,256]{2,1,0:T(8,128)(2,1)}, u32[]{:S(2)}) copy-start(bf16[8,512,256]{2,1,0:T(8,128)(2,1)} %constant.10.clone.table_hbm.tables_hbm.table_ref) | copy-start | bytes 6291460
  56.9 31.3 %copy-start.1 = (s32[256,8,256]{2,1,0:T(8,128)S(1)}, s32[256,8,256]{2,1,0:T(8,128)}, u32[]{:S(2)}) copy-start(s32[256,8,256]{2,1,0:T(8,128)} %mask_ref.1) | copy-start | bytes 6291460
  103.6 5.3 %collective-permute-start.1 = (f32[1,128]{1,0:T(1,128)S(1)}, f32[1,128]{1,0:T(1,128)S(1)}, u32[]{:S(2)}, u32[]{:S(2)}) collective-permute-start(f32[1,128]{1,0:T(1,128)S(1)} %bitcast.9), channel_id=1, source_target_pairs={{0,32},{32,64},{64,96},{96,0},{1,33},{33,65},{65,97},{97,1},{2,34}... | collective-permute-start | bytes 1544 | tf_op jit(solution)/shard_map/ppermute | solution.py:432
  105.2 3.7 %collective-permute-start.2 = (f32[1,128]{1,0:T(1,128)S(1)}, f32[1,128]{1,0:T(1,128)S(1)}, u32[]{:S(2)}, u32[]{:S(2)}) collective-permute-start(f32[1,128]{1,0:T(1,128)S(1)} %bitcast.10), channel_id=1, source_target_pairs={{0,96},{32,0},{64,32},{96,64},{1,97},{33,1},{65,33},{97,65},{2,98}... | collective-permute-start | bytes 1544 | tf_op jit(solution)/shard_map/ppermute | solution.py:432
  106.8 5.1 %collective-permute-start = (f32[1,128]{1,0:T(1,128)S(1)}, f32[1,128]{1,0:T(1,128)S(1)}, u32[]{:S(2)}, u32[]{:S(2)}) collective-permute-start(f32[1,128]{1,0:T(1,128)S(1)} %bitcast.11), channel_id=1, source_target_pairs={{0,64},{32,96},{64,0},{96,32},{1,65},{33,97},{65,1},{97,33},{2,66}... | collective-permute-start | bytes 1544 | tf_op jit(solution)/shard_map/ppermute | solution.py:432
